TPU v7x, 32 devices: a whole 2x2x4 slice. The times are simulated.
32 devices in a mesh: grp: 4 (over z), fsdp: 4 (over y, x), tp: 2 (over core).
Axes of the slice: x: 2, y: 2, z: 4, core: 2. Of those that a mesh axis runs over, the one named last changes fastest.
Arguments:
- frames: bfloat16 [768, 5120], P('fsdp', 'grp'), may hold values from -6 to 6
- projector: bfloat16 [5120, 8192], P('grp', 'tp'), may hold values from -0.078125 to 0.078125
- text_token_embedding: bfloat16 [4096, 8192], P(('grp', 'fsdp'), 'tp'), may hold values from -6 to 6
- norm_gain_vector: float32 [8192], replicated, may hold values from 0.1 to 1.9
- frozen: bfloat16 [8192, 1024], P('fsdp', 'tp'), may hold values from -0.0625 to 0.0625
- adapter_down_map: bfloat16 [8192, 64], P('fsdp'), may hold values from -0.0625 to 0.0625
- adapter_up_map: bfloat16 [64, 1024], P(None, 'tp'), may hold values from -0.75 to 0.75
- clip_frame_length: int32 [4, 4, 4], P('fsdp'), may hold values from 1 to 24, as said below
- audio_first_token: int32 [4, 4, 4], P('fsdp'), may hold values from 0 to 255, as said below
- segment_document_index: int32 [4096], P(('grp', 'fsdp')), may hold values from 0 to 63, never falling along the last dimension, each value on 1 to 256 neighbouring positions
- keep_document_flags: int32 [64], replicated, may hold values 0 or 1
- cotangent: bfloat16 [4096, 1024], P(('grp', 'fsdp'), 'tp'), may hold values from -0.09375 to 0.09375
Outputs:
- value_output: bfloat16 [4096, 1024], P(('grp', 'fsdp'), 'tp')
- projector_grad: float32 [5120, 8192], P('grp', 'tp')
- down_map_gradient: float32 [8192, 64], P('tp')
- up_map_gradient: float32 [64, 1024], P(None, 'tp')
Inputs may be any that keep to these rules, and one draw needn't show every extreme that they name: `clip_frame_length`: entry [f, g, k] is the length of clip k of frame block f * 4 + g; the 4 clips of a block sum to 48, and one of them has exactly 24 frames. `audio_first_token`: entry [f, g, k] is the first token, among the 256 tokens of block k * 4 + f, of the audio slots of clip k of frame block f * 4 + g; the 4 clips that one token block takes lie in distinct aligned windows of 64 tokens.
All inputs are finite; a program needn't handle non-finite values.
Results may differ from a plain program's by a relative error of at most 0.018.
Values may be sent and summed in bfloat16 or wider, within the bound.
A program may use at most 128 MiB of HBM per device.

v0:
```python
import jax
import jax.numpy as jnp
from jax import lax
from jax.sharding import PartitionSpec as P

adapter_scale = 2.0
norm_eps = 1e-05


def pick_entry(grid_in, position, which_axis):
    matches = lax.broadcasted_iota(jnp.int32, grid_in.shape, which_axis) == position
    return jnp.sum(jnp.where(matches, grid_in, 0), axis=which_axis)


def contract_leading(left_side, right_side):
    return lax.dot_general(
        left_side, right_side, (((0,), (0,)), ((), ())), preferred_element_type=jnp.float32
    )


def contract_trailing(left_side, right_side):
    return lax.dot_general(
        left_side, right_side, (((1,), (1,)), ((), ())), preferred_element_type=jnp.float32
    )


def shards(
    frames,
    projector,
    text_token_embedding,
    norm_gain_vector,
    frozen,
    adapter_down_map,
    adapter_up_map,
    clip_frame_length,
    audio_first_token,
    segment_document_index,
    keep_document_flags,
    cotangent,
):
    grp_index = lax.axis_index("grp")
    tensor_shard_index = lax.axis_index("tp")
    tok_count, tensor_shard_width = text_token_embedding.shape
    group_count = clip_frame_length.shape[1]
    frame_count = frames.shape[0] // group_count
    slot_cap = 2 * frame_count // group_count
    slot_total = group_count * slot_cap
    full_width = tensor_shard_width * lax.axis_size("tp")
    own_sizes = pick_entry(clip_frame_length[0], grp_index, 0)
    own_starts = jnp.cumsum(own_sizes) - own_sizes
    slot_offset = lax.broadcasted_iota(jnp.int32, (group_count, slot_cap), 1)
    frame_slot = own_starts[:, None] + slot_offset
    slot_live = slot_offset < own_sizes[:, None]
    frame_iota = lax.broadcasted_iota(jnp.int32, (group_count, slot_cap, frame_count), 2)
    sender = (
        ((frame_iota == frame_slot[:, :, None]) & slot_live[:, :, None])
        .astype(jnp.bfloat16)
        .reshape(slot_total, frame_count)
    )
    in_sizes = pick_entry(clip_frame_length[0], grp_index, 1)
    arrive_at = pick_entry(audio_first_token[0], grp_index, 1)
    token_iota = lax.broadcasted_iota(jnp.int32, (tok_count, group_count, slot_cap), 0)
    receive_mask = (token_iota == (arrive_at[:, None] + slot_offset)[None]) & (
        slot_offset < in_sizes[:, None]
    )[None]
    receiving_device = receive_mask.astype(jnp.bfloat16).reshape(tok_count, slot_total)
    is_audio = jnp.any(receive_mask, axis=(1, 2))
    embedded = lax.psum_scatter(
        jnp.dot(frames, projector, preferred_element_type=jnp.float32).astype(jnp.bfloat16),
        "grp",
        scatter_dimension=0,
        tiled=True,
    )
    outgoing = (
        jnp.dot(sender, embedded, preferred_element_type=jnp.float32)
        .astype(jnp.bfloat16)
        .reshape(group_count, slot_cap, tensor_shard_width)
    )
    incoming = lax.all_to_all(outgoing, "grp", split_axis=0, concat_axis=0, tiled=True).reshape(
        slot_total, tensor_shard_width
    )
    audio_part = jnp.dot(receiving_device, incoming, preferred_element_type=jnp.float32).astype(
        jnp.bfloat16
    )
    inputs = jnp.where(is_audio[:, None], audio_part, text_token_embedding)
    gathered = lax.all_gather(inputs, "tp", axis=1, tiled=True)
    widened = gathered.astype(jnp.float32)
    mean_sq = jnp.mean(widened * widened, axis=1)
    inv_rms = lax.rsqrt(mean_sq + norm_eps)
    normalized_input = (widened * inv_rms[:, None] * norm_gain_vector[None, :]).astype(jnp.bfloat16)
    frozen_complete, adapter_complete = (
        lax.all_gather(frozen, "fsdp", axis=0, tiled=True),
        lax.all_gather(adapter_down_map, "fsdp", axis=0, tiled=True),
    )
    base_output = jnp.dot(normalized_input, frozen_complete, preferred_element_type=jnp.float32)
    lower_rank_rows = jnp.dot(
        normalized_input, adapter_complete, preferred_element_type=jnp.float32
    )
    lower_halfway = lower_rank_rows.astype(jnp.bfloat16)
    value_output = (
        base_output
        + adapter_scale * jnp.dot(lower_halfway, adapter_up_map, preferred_element_type=jnp.float32)
    ).astype(jnp.bfloat16)
    doc_iota = lax.broadcasted_iota(jnp.int32, (tok_count, keep_document_flags.shape[0]), 1)
    weight_tok = jnp.sum(
        jnp.where(segment_document_index[:, None] == doc_iota, keep_document_flags[None, :], 0),
        axis=1,
    )
    output_gradient = cotangent * weight_tok.astype(jnp.bfloat16)[:, None]
    adapter_portion = adapter_scale * contract_trailing(output_gradient, adapter_up_map)
    dot_portion = jnp.sum(output_gradient.astype(jnp.float32) * base_output, axis=1) + jnp.sum(
        adapter_portion * lower_rank_rows, axis=1
    )
    adapter_gradient, row_dot_products = (
        lax.psum(adapter_portion.astype(jnp.bfloat16), "tp").astype(jnp.float32),
        lax.psum(dot_portion.astype(jnp.bfloat16), "tp").astype(jnp.float32),
    )
    adapter_halfway = adapter_gradient.astype(jnp.bfloat16)
    up_portion = adapter_scale * contract_leading(lower_halfway, output_gradient)
    local_normalized = lax.dynamic_slice_in_dim(
        normalized_input, tensor_shard_index * tensor_shard_width, tensor_shard_width, 1
    )
    down_portion = contract_leading(local_normalized, adapter_halfway)
    down_map_gradient, up_map_gradient = lax.psum((down_portion, up_portion), ("grp", "fsdp"))
    slot_grad = contract_leading(receiving_device, output_gradient).astype(jnp.bfloat16)
    slot_adapter = contract_leading(receiving_device, adapter_halfway).astype(jnp.bfloat16)
    slot_stats = lax.dot_general(
        receiving_device.astype(jnp.float32),
        jnp.stack([inv_rms, row_dot_products], axis=1),
        (((0,), (0,)), ((), ())),
        precision=lax.Precision.HIGHEST,
        preferred_element_type=jnp.float32,
    )
    spread_rows = contract_trailing(slot_grad, frozen_complete)
    reduced_result = lax.psum_scatter(
        spread_rows.astype(jnp.bfloat16), "tp", scatter_dimension=1, tiled=True
    ).astype(jnp.float32)
    local_adapter = lax.dynamic_slice_in_dim(
        adapter_complete, tensor_shard_index * tensor_shard_width, tensor_shard_width, 0
    )
    gradient_norm = reduced_result + contract_trailing(slot_adapter, local_adapter)
    own_gain = lax.dynamic_slice_in_dim(
        norm_gain_vector, tensor_shard_index * tensor_shard_width, tensor_shard_width, 0
    )
    slot_inv = slot_stats[:, 0:1]
    slot_dot = slot_stats[:, 1:2]
    grad_rows = (
        slot_inv * own_gain[None, :] * gradient_norm
        - incoming.astype(jnp.float32) * (slot_inv * slot_inv * slot_dot / full_width)
    ).astype(jnp.bfloat16)
    returned = lax.all_to_all(
        grad_rows.reshape(group_count, slot_cap, tensor_shard_width),
        "grp",
        split_axis=0,
        concat_axis=0,
        tiled=True,
    ).reshape(slot_total, tensor_shard_width)
    frame_grad = contract_leading(sender, returned).astype(jnp.bfloat16)
    proj_part = contract_leading(frames, lax.all_gather(frame_grad, "grp", axis=0, tiled=True))
    projector_grad = lax.psum(proj_part.astype(jnp.bfloat16), "fsdp").astype(jnp.float32)
    return (value_output, projector_grad, down_map_gradient, up_map_gradient)


def solution(mesh):
    in_specs = (
        P("fsdp", "grp"),
        P("grp", "tp"),
        P(("grp", "fsdp"), "tp"),
        P(),
        P("fsdp", "tp"),
        P("fsdp", None),
        P(None, "tp"),
        P("fsdp", None, None),
        P("fsdp", None, None),
        P(("grp", "fsdp")),
        P(),
        P(("grp", "fsdp"), "tp"),
    )
    out_specs = (P(("grp", "fsdp"), "tp"), P("grp", "tp"), P("tp", None), P(None, "tp"))
    return jax.shard_map(shards, mesh=mesh, in_specs=in_specs, out_specs=out_specs, check_vma=False)
```

profile of v0, /device:TPU:0, one launch (start us, length us, event | category | flops | bytes accessed | tf_op | source)
XLA Modules:
  0.0 638.0 jit_solution(16434145417665947349)
XLA Ops:
  7.2 1.0 copy-done
  8.2 7.3 %convolution_convert_fusion.2 = bf16[192,4096]{1,0:T(8,128)(2,1)} fusion(bf16[192,1280]{1,0:T(8,128)(2,1)S(1)} %copy-done, bf16[1280,4096]{1,0:T(8,128)(2,1)} %param.13), kind=kOutput, calls=%fused_computation.10 | convolution fusion | flops 2014052352 | bytes 12550144 | tf_op jit(solution)/shard_map/dot_general | solution.py:69
  16.7 37.2 %reduce-scatter.3.cloned.1.call-done = bf16[48,4096]{1,0:T(8,128)(2,1)} async-done(((bf16[192,4096]{1,0:T(8,128)(2,1)}), bf16[48,4096]{1,0:T(8,128)(2,1)}) %reduce-scatter.3.cloned.1.call-update) | async-done | bytes 393232 | tf_op jit(solution)/shard_map/reduce_scatter | solution.py:68
  53.9 2.3 convolution_convert_fusion.3
  56.2 3.5 all-to-all-start
  60.0 19.6 %all-to-all-done = bf16[4,24,4096]{2,1,0:T(8,128)(2,1)S(1)} async-done(((bf16[4,24,4096]{2,1,0:T(8,128)(2,1)}), bf16[4,24,4096]{2,1,0:T(8,128)(2,1)S(1)}, u32[]{:S(2)}, u32[]{:S(2)}) %all-to-all-start) | async-done | bytes 786464 | tf_op jit(solution)/shard_map/all_to_all | solution.py:79
  79.7 3.7 fusion.8
  83.5 0.7 all-gather.7.cloned.1.call-update
  84.2 0.5 all-gather.9.cloned.1.call-update
  84.9 11.4 %all-gather.5.cloned.1.call-done = bf16[256,8192]{1,0:T(8,128)(2,1)} async-done(((bf16[256,4096]{1,0:T(8,128)(2,1)}), bf16[256,8192]{1,0:T(8,128)(2,1)}) %all-gather.5.cloned.1.call-update) | async-done | bytes 4194320 | tf_op jit(solution)/shard_map/all_gather | solution.py:86
  96.3 3.1 fusion.1
  99.4 87.4 %all-gather.7.cloned.1.call-done = bf16[8192,512]{1,0:T(8,128)(2,1)} async-done(((bf16[2048,512]{1,0:T(8,128)(2,1)}), bf16[8192,512]{1,0:T(8,128)(2,1)}) %all-gather.7.cloned.1.call-update) | async-done | bytes 8388624 | tf_op jit(solution)/shard_map/all_gather | solution.py:92
  186.8 7.4 %convolution_convert_fusion.1 = bf16[96,8192]{1,0:T(8,128)(2,1)} fusion(bf16[8192,512]{1,0:T(8,128)(2,1)} %all-gather.7.cloned.1.call-done, bf16[256,512]{1,0:T(8,128)(2,1)S(1)} %copy-done.4, bf16[256]{0:T(256)(128)(2,1)S(1)} %convert_element_type.83, s32[96]{0:T(128)S(1)} %get-tuple-element.29, pred[96]{0:T(512)(128)(4,1)S(1)} %get-tuple-element.27), kind=kOutput, calls=%fused_computation.4 | convolution fusion | flops 831488000 | bytes 10224608 | tf_op jit(solution)/shard_map/dot_general | solution.py:22
  194.2 5.5 fusion.3
  199.7 15.4 %all-gather.9.cloned.1.call-done = bf16[8192,64]{0,1:T(8,128)(2,1)} async-done(((bf16[2048,64]{0,1:T(8,128)(2,1)}), bf16[8192,64]{0,1:T(8,128)(2,1)}) %all-gather.9.cloned.1.call-update) | async-done | bytes 1048592 | tf_op jit(solution)/shard_map/all_gather | solution.py:93
  215.1 4.0 fusion.66
  219.4 5.9 multiply_reduce_fusion
  225.3 3.5 all-reduce.1
  229.0 2.8 fusion.7
  231.8 4.6 all-to-all-start.1
  236.5 20.5 %all-to-all-done.1 = bf16[4,24,4096]{2,1,0:T(8,128)(2,1)S(1)} async-done(((bf16[4,24,4096]{2,1,0:T(8,128)(2,1)}), bf16[4,24,4096]{2,1,0:T(8,128)(2,1)S(1)}, u32[]{:S(2)}, u32[]{:S(2)}) %all-to-all-start.1) | async-done | bytes 786464 | tf_op jit(solution)/shard_map/all_to_all | solution.py:151
  257.0 1.1 fusion.9
  258.4 35.1 %all-gather.11.cloned.1.call-done = bf16[192,4096]{1,0:T(8,128)(2,1)} async-done(((bf16[48,4096]{1,0:T(8,128)(2,1)}), bf16[192,4096]{1,0:T(8,128)(2,1)}) %all-gather.11.cloned.1.call-update) | async-done | bytes 1572880 | tf_op jit(solution)/shard_map/all_gather | solution.py:159
  293.5 8.5 %fusion = bf16[1280,4096]{0,1:T(8,128)(2,1)} fusion(bf16[192,4096]{1,0:T(8,128)(2,1)} %all-gather.11.cloned.1.call-done, bf16[192,1280]{1,0:T(8,128)(2,1)S(1)} %copy-done), kind=kOutput, calls=%fused_computation.1 | convolution fusion | flops 2018508800 | bytes 12550144 | tf_op jit(solution)/shard_map/dot_general | solution.py:16
  302.0 0.9 convolution_multiply_fusion.1
  302.9 3.0 fusion.10
  305.9 1.0 fusion.13
  306.9 200.3 %all-reduce.5.cloned.1.call-done = bf16[1280,4096]{0,1:T(8,128)(2,1)} async-done(((bf16[1280,4096]{0,1:T(8,128)(2,1)}), bf16[1280,4096]{0,1:T(8,128)(2,1)}) %all-reduce.5.cloned.1.call-update) | async-done | bytes 10485776 | tf_op jit(solution)/shard_map/psum | solution.py:160
  507.2 16.1 %copy.18 = f32[1280,4096]{1,0:T(8,128)} copy(bf16[1280,4096]{0,1:T(8,128)(2,1)} %all-reduce.5.cloned.1.call-done) | data formatting | bytes 31457280
  523.2 104.1 %all-reduce.7.cloned.1.call-done = (f32[4096,64]{0,1:T(8,128)}, f32[64,512]{1,0:T(8,128)}) async-done(((f32[4096,64]{0,1:T(8,128)}, f32[64,512]{1,0:T(8,128)}), (f32[4096,64]{0,1:T(8,128)}, f32[64,512]{1,0:T(8,128)})) %all-reduce.7.cloned.1.call-update) | async-done | bytes 1179664 | tf_op jit(solution)/shard_map/psum | solution.py:124
  627.3 2.3 copy.22
  629.6 1.6 copy.23
  (68 shorter events, 2.7 us)
Async XLA Ops:
  7.2 1.0 copy-start
  7.2 8.4 %copy-start.7 = (s32[1,4,4]{2,1,0:T(4,128)S(1)}, s32[1,4,4]{2,1,0:T(4,128)}, u32[]{:S(2)}) copy-start(s32[1,4,4]{2,1,0:T(4,128)} %param.19) | copy-start | bytes 196
  7.2 8.4 %copy-start.8 = (s32[1,4,4]{2,1,0:T(4,128)S(1)}, s32[1,4,4]{2,1,0:T(4,128)}, u32[]{:S(2)}) copy-start(s32[1,4,4]{2,1,0:T(4,128)} %param.20) | copy-start | bytes 196
  7.2 46.7 %reduce-scatter.3.cloned.1.call-start = ((), (), s32[]{:S(2)}) async-start(), calls=%async_computation.4 | async-start | bytes 1966080 | tf_op jit(solution)/shard_map/reduce_scatter | solution.py:68
  56.2 23.5 %all-to-all-start = ((bf16[4,24,4096]{2,1,0:T(8,128)(2,1)}), bf16[4,24,4096]{2,1,0:T(8,128)(2,1)S(1)}, u32[]{:S(2)}, u32[]{:S(2)}) async-start(bf16[4,24,4096]{2,1,0:T(8,128)(2,1)} %bitcast.4), calls=%async_computation.1 | async-start | bytes 1572864 | tf_op jit(solution)/shard_map/all_to_all | solution.py:79
  59.7 36.6 %all-gather.5.cloned.1.call-start = ((), (), s32[]{:S(2)}) async-start(), calls=%async_computation.5 | async-start | bytes 6291456 | tf_op jit(solution)/shard_map/all_gather | solution.py:86
  60.0 24.8 %copy-start.9 = (s32[256]{0:T(256)S(1)}, s32[256]{0:T(256)}, u32[]{:S(2)}) copy-start(s32[256]{0:T(256)} %param.21) | copy-start | bytes 3076
  60.0 24.8 %copy-start.10 = (s32[64]{0:T(128)S(1)}, s32[64]{0:T(128)}, u32[]{:S(2)}) copy-start(s32[64]{0:T(128)} %param.22) | copy-start | bytes 772
  83.4 103.4 %copy-start.4 = (bf16[256,512]{1,0:T(8,128)(2,1)S(1)}, bf16[256,512]{1,0:T(8,128)(2,1)}, u32[]{:S(2)}) copy-start(bf16[256,512]{1,0:T(8,128)(2,1)} %param.23) | copy-start | bytes 786436
  83.4 103.4 %all-gather.7.cloned.1.call-start = ((), (), s32[]{:S(2)}) async-start(), calls=%async_computation.6 | async-start | bytes 10485760 | tf_op jit(solution)/shard_map/all_gather | solution.py:92
  84.2 130.9 %all-gather.9.cloned.1.call-start = ((), (), s32[]{:S(2)}) async-start(), calls=%async_computation.7 | async-start | bytes 1310720 | tf_op jit(solution)/shard_map/all_gather | solution.py:93
  84.8 144.2 %reduce-scatter.5.cloned.1.call-start = ((), (), s32[]{:S(2)}) async-start(), calls=%async_computation.8 | async-start | bytes 2359296 | tf_op jit(solution)/shard_map/reduce_scatter | solution.py:135
  186.8 7.4 %copy-start.5 = (f32[8192]{0:T(1024)S(1)}, f32[8192]{0:T(1024)}, u32[]{:S(2)}) copy-start(f32[8192]{0:T(1024)} %param.15) | copy-start | bytes 98308
  199.7 19.4 %copy-start.6 = (bf16[64,512]{1,0:T(8,128)(2,1)S(1)}, bf16[64,512]{1,0:T(8,128)(2,1)}, u32[]{:S(2)}) copy-start(bf16[64,512]{1,0:T(8,128)(2,1)} %param.18) | copy-start | bytes 196612
  215.1 4.3 copy-start.2
  219.4 9.6 %copy-start.3 = (bf16[8192,64]{0,1:T(8,128)(2,1)S(1)}, bf16[8192,64]{0,1:T(8,128)(2,1)}, u32[]{:S(2)}) copy-start(bf16[8192,64]{0,1:T(8,128)(2,1)} %all-gather.9.cloned.1.call-done) | copy-start | bytes 3145732
  219.4 9.6 %dynamic-slice-start = ((f32[8192]{0:T(1024)}, s32[]{:T(128)}), f32[4096]{0:T(1024)S(1)}, s32[]{:S(2)}) async-start(f32[8192]{0:T(1024)} %param.15, s32[]{:T(128)} %select_n.28), calls=%async_computation.12 | async-start | bytes 33280 | tf_op jit(solution)/shard_map/dynamic_slice | solution.py:142
  231.8 25.2 %all-to-all-start.1 = ((bf16[4,24,4096]{2,1,0:T(8,128)(2,1)}), bf16[4,24,4096]{2,1,0:T(8,128)(2,1)S(1)}, u32[]{:S(2)}, u32[]{:S(2)}) async-start(bf16[4,24,4096]{2,1,0:T(8,128)(2,1)} %bitcast.10), calls=%async_computation.3 | async-start | bytes 1572864 | tf_op jit(solution)/shard_map/all_to_all | solution.py:151
  236.4 57.1 %all-gather.11.cloned.1.call-start = ((), (), s32[]{:S(2)}) async-start(), calls=%async_computation.9 | async-start | bytes 1966080 | tf_op jit(solution)/shard_map/all_gather | solution.py:159
  258.1 249.0 %all-reduce.5.cloned.1.call-start = ((), (), s32[]{:S(2)}) async-start(), calls=%async_computation.10 | async-start | bytes 20971520 | tf_op jit(solution)/shard_map/psum | solution.py:160
  301.9 325.4 %all-reduce.7.cloned.1.call-start = ((), (), s32[]{:S(2)}) async-start(), calls=%async_computation.11 | async-start | bytes 2359296 | tf_op jit(solution)/shard_map/psum | solution.py:124
  507.2 124.0 %copy-start.1 = (bf16[192,1280]{1,0:T(8,128)(2,1)S(1)}, bf16[192,1280]{1,0:T(8,128)(2,1)}, u32[]{:S(2)}) copy-start(bf16[192,1280]{1,0:T(8,128)(2,1)} %param.12) | copy-start | bytes 1474564
Sparse Core Ops, SparseCore 0:
  15.7 38.1 reduce-scatter.2
  83.6 12.6 all-gather.4
  98.1 88.6 all-gather.6
  188.5 26.4 all-gather.8
  217.7 8.9 reduce-scatter.4
  258.3 35.1 all-gather.10
  302.1 205.0 all-reduce.4
  513.2 114.1 all-reduce.6
where the time goes:
time: 639 us; the launch traced here: 638 us
  waiting for transfers between devices  532 us (83%)
  matrix products  48.3 us (8%)
  local copies, waits for them, and re-layouts  21.6 us (3%)
  between operations  14.4 us (2%)
  other arithmetic  9.44 us (1%)
  starting transfers between devices  8.56 us (1%)
    psum x1, waiting for transfers between devices, shards(): lax.psum(proj_part.astype(jnp.bfloat16), 'fsdp').astype(jnp.float32)  200 us
    psum x1, waiting for transfers between devices, shards(): lax.psum((down_portion, up_portion), ('grp', 'fsdp'))  104 us
    all_gather x1, waiting for transfers between devices, shards(): lax.all_gather(frozen, 'fsdp', axis=0, tiled=True)  87.4 us
    reduce_scatter x1, waiting for transfers between devices, shards(): lax.psum_scatter(jnp.dot(frames, projector, preferred_element_type=jnp.fl...  37.2 us
    all_gather x1, waiting for transfers between devices, shards(): lax.all_gather(frame_grad, 'grp', axis=0, tiled=True)  35.1 us
    unnamed x25, local copies, waits for them, and re-layouts  20.9 us
    all_to_all x1, waiting for transfers between devices, shards(): lax.all_to_all(grad_rows.reshape(group_count, slot_cap, tensor_shard_widt...  20.5 us
    all_to_all x1, waiting for transfers between devices, shards(): lax.all_to_all(outgoing, 'grp', split_axis=0, concat_axis=0, tiled=True)  19.6 us
  transfers between devices with their start and end apart: 10, of which 9 were waited for; matrix products, arithmetic and copies ran while one was open for 8% of the time, Pallas kernels for 0%

commit v1 on v0

v1 whole, which is shorter than its diff:
```python
import jax
import jax.numpy as jnp
from jax import lax
from jax.sharding import PartitionSpec as P

adapter_scale = 2.0
norm_eps = 1e-05
plane = ("fsdp", "tp")


def contract_leading(left_side, right_side):
    return lax.dot_general(
        left_side, right_side, (((0,), (0,)), ((), ())), preferred_element_type=jnp.float32
    )


def contract_trailing(left_side, right_side):
    return lax.dot_general(
        left_side, right_side, (((1,), (1,)), ((), ())), preferred_element_type=jnp.float32
    )


def block_perm(f_size, t_size, shift):
    pairs = []
    for f_src in range(f_size):
        for t_src in range(t_size):
            b = f_src * t_size + (t_src + shift) % t_size
            pairs.append((f_src * t_size + t_src, (b % f_size) * t_size + b // f_size))
    return pairs


def shards(
    frames,
    projector,
    text_token_embedding,
    norm_gain_vector,
    frozen,
    adapter_down_map,
    adapter_up_map,
    clip_frame_length,
    audio_first_token,
    segment_document_index,
    keep_document_flags,
    cotangent,
):
    g_idx, f_idx, t_idx = lax.axis_index("grp"), lax.axis_index("fsdp"), lax.axis_index("tp")
    f_size, t_size = lax.axis_size("fsdp"), lax.axis_size("tp")
    tok, width = text_token_embedding.shape
    groups = clip_frame_length.shape[1]
    block_frames = frames.shape[0]
    per_group = block_frames // groups
    cols = width // f_size
    full_width = width * t_size
    v_shard = frozen.shape[1]
    v_full = v_shard * t_size
    rank = adapter_down_map.shape[1]

    frames_all = lax.all_gather(frames, "fsdp", axis=0, tiled=True)
    clips = lax.all_gather(jnp.stack([clip_frame_length[0], audio_first_token[0]]), "fsdp", axis=0)
    text = lax.all_to_all(
        text_token_embedding.reshape(tok, f_size, cols).transpose(1, 0, 2),
        "fsdp",
        split_axis=0,
        concat_axis=0,
        tiled=True,
    )

    own_block = t_idx * f_size + f_idx
    own_j = lax.rem(own_block, t_size)
    frozen_own = jnp.zeros((cols, v_full), jnp.bfloat16)
    for shift in range(t_size):
        j = lax.rem(t_idx + shift, t_size)
        piece = lax.ppermute(
            lax.dynamic_slice_in_dim(frozen, j * cols, cols, 0),
            plane,
            block_perm(f_size, t_size, shift),
        )
        t_src = lax.rem(own_j - shift + t_size, t_size)
        frozen_own = lax.dynamic_update_slice_in_dim(frozen_own, piece, t_src * v_shard, 1)
    down_own = lax.ppermute(
        lax.dynamic_slice_in_dim(adapter_down_map, t_idx * cols, cols, 0),
        plane,
        block_perm(f_size, t_size, 0),
    )
    gain_own = lax.dynamic_slice_in_dim(norm_gain_vector, t_idx * width + f_idx * cols, cols, 0)

    sizes, firsts = clips[:, 0], clips[:, 1]
    ends = jnp.cumsum(sizes, axis=2)
    pick = lax.broadcasted_iota(jnp.int32, sizes.shape, 2) == g_idx
    size_in = jnp.sum(jnp.where(pick, sizes, 0), axis=2)
    start_in = jnp.sum(jnp.where(pick, ends - sizes, 0), axis=2)
    first_in = jnp.sum(jnp.where(pick, firsts, 0), axis=2)
    base_row = lax.broadcasted_iota(jnp.int32, size_in.shape, 1) * per_group + start_in
    token_iota = lax.broadcasted_iota(jnp.int32, (f_size, tok, groups), 1)
    offset = token_iota - first_in[:, None, :]
    live = (offset >= 0) & (offset < size_in[:, None, :])
    is_audio = jnp.any(live, axis=2)
    row = jnp.sum(jnp.where(live, base_row[:, None, :] + offset, 0), axis=2)
    row = jnp.where(is_audio, row, -1)
    frame_iota = lax.broadcasted_iota(jnp.int32, (f_size, tok, block_frames), 2)
    take = (row[:, :, None] == frame_iota).astype(jnp.bfloat16)
    take_own = lax.dynamic_index_in_dim(take, f_idx, 0, keepdims=False)

    doc_iota = lax.broadcasted_iota(jnp.int32, (tok, keep_document_flags.shape[0]), 1)
    weight_tok = jnp.sum(
        jnp.where(segment_document_index[:, None] == doc_iota, keep_document_flags[None, :], 0),
        axis=1,
    )
    grad_out = cotangent * weight_tok.astype(jnp.bfloat16)[:, None]
    both = lax.all_gather(
        jnp.concatenate([grad_out, adapter_up_map], axis=0), "tp", axis=1, tiled=True
    )
    grad_full, up_full = both[:tok], both[tok:]
    lora_tok = (adapter_scale * contract_trailing(grad_full, up_full)).astype(jnp.bfloat16)
    lora_plane = lax.all_gather(lora_tok, "fsdp", axis=0, tiled=True)
    grad_rows = lax.psum(contract_leading(take_own, grad_full).astype(jnp.bfloat16), "grp")
    grad_rows = lax.all_gather(grad_rows, "fsdp", axis=0, tiled=True)
    lora_rows = (adapter_scale * contract_trailing(grad_rows, up_full)).astype(jnp.bfloat16)
    grad_norm = contract_trailing(grad_rows, frozen_own) + contract_trailing(lora_rows, down_own)

    projector_own = lax.dynamic_slice_in_dim(projector, f_idx * cols, cols, 1)
    embedded = lax.psum(
        jnp.dot(frames_all, projector_own, preferred_element_type=jnp.float32).astype(jnp.bfloat16),
        "grp",
    )
    audio = lax.dot_general(
        take,
        embedded.reshape(f_size, block_frames, cols),
        (((2,), (1,)), ((0,), (0,))),
        preferred_element_type=jnp.float32,
    ).astype(jnp.bfloat16)
    x = jnp.where(is_audio[:, :, None], audio, text).reshape(f_size * tok, cols)
    x32 = x.astype(jnp.float32)
    e32 = embedded.astype(jnp.float32)
    stats = lax.psum(
        jnp.concatenate(
            [
                jnp.sum(x32 * x32, axis=1),
                jnp.sum(e32 * e32, axis=1),
                jnp.sum(e32 * gain_own[None, :] * grad_norm, axis=1),
            ]
        ),
        plane,
    )
    n_tok, n_frames = f_size * tok, f_size * block_frames
    inv_tok = lax.rsqrt(stats[:n_tok] / full_width + norm_eps)
    inv_frame = lax.rsqrt(stats[n_tok : n_tok + n_frames] / full_width + norm_eps)
    dots = inv_frame * stats[n_tok + n_frames :]
    frame_grad = (
        (inv_frame[:, None] * gain_own[None, :]) * grad_norm
        - e32 * (inv_frame * inv_frame * dots / full_width)[:, None]
    ).astype(jnp.bfloat16)
    frame_grad = lax.all_gather(frame_grad, "fsdp", axis=1, tiled=True)
    projector_grad = contract_leading(frames_all, frame_grad)

    normed = (x32 * inv_tok[:, None] * gain_own[None, :]).astype(jnp.bfloat16)
    low_part = jnp.dot(normed, down_own, preferred_element_type=jnp.float32)
    value_part = jnp.dot(normed, frozen_own, preferred_element_type=jnp.float32)
    value_part = value_part + adapter_scale * jnp.dot(
        low_part.astype(jnp.bfloat16), up_full, preferred_element_type=jnp.float32
    )
    value_part = value_part.astype(jnp.bfloat16).reshape(f_size, tok, t_size, v_shard)
    low_send = jnp.broadcast_to(
        low_part.astype(jnp.bfloat16).reshape(f_size, tok, 1, rank), (f_size, tok, t_size, rank)
    )
    sent = (
        jnp.concatenate([value_part, low_send], axis=3)
        .transpose(0, 2, 1, 3)
        .reshape(f_size * t_size, tok, v_shard + rank)
    )
    got = lax.all_to_all(sent, plane, split_axis=0, concat_axis=0, tiled=True)
    total = jnp.sum(got.astype(jnp.float32), axis=0)
    value_output = total[:, :v_shard].astype(jnp.bfloat16)
    low_half = total[:, v_shard:].astype(jnp.bfloat16)

    up_part = adapter_scale * contract_leading(low_half, grad_out)
    down_part = contract_leading(normed, lora_plane)
    down_sum, up_sum = lax.psum((down_part, up_part), "grp")
    gathered = lax.all_gather(
        jnp.concatenate([down_sum, up_sum.reshape(-1, rank)], axis=0), "fsdp", axis=0
    )
    down_map_gradient = gathered[:, :cols].reshape(width, rank)
    up_map_gradient = jnp.sum(gathered[:, cols:], axis=0).reshape(rank, v_shard)
    return (value_output, projector_grad, down_map_gradient, up_map_gradient)


def solution(mesh):
    in_specs = (
        P("fsdp", "grp"),
        P("grp", "tp"),
        P(("grp", "fsdp"), "tp"),
        P(),
        P("fsdp", "tp"),
        P("fsdp", None),
        P(None, "tp"),
        P("fsdp", None, None),
        P("fsdp", None, None),
        P(("grp", "fsdp")),
        P(),
        P(("grp", "fsdp"), "tp"),
    )
    out_specs = (P(("grp", "fsdp"), "tp"), P("grp", "tp"), P("tp", None), P(None, "tp"))
    return jax.shard_map(shards, mesh=mesh, in_specs=in_specs, out_specs=out_specs, check_vma=False)
```

time: 639 us -> 502 us (0.79)
  waiting for transfers between devices: 532 us -> 273 us
  blocking collectives: 3.46 us -> 71.6 us
  local copies, waits for them, and re-layouts: 21.6 us -> 58.1 us
  starting transfers between devices: 8.56 us -> 18.6 us
  other arithmetic: 9.44 us -> 18.5 us
    psum x2, waiting for transfers between devices: 304 us -> 118 us  [the longest x1 82 us: shards(): lax.psum(jnp.dot(frames_all, projector_own, preferred_element_type=jnp.fl...]
    all_gather x0 -> x3, blocking collectives: none -> 44.4 us  [the longest x1 32.5 us: shards(): lora_plane = lax.all_gather(lora_tok, 'fsdp', axis=0, tiled=True)]
    all_to_all x2, waiting for transfers between devices: 40.1 us -> 0.01 us  [the longest x1 0.01 us: shards(): lax.all_to_all(text_token_embedding.reshape(tok, f_size, cols).transpose(...]
    ppermute x0 -> x3, waiting for transfers between devices: none -> 40.1 us  [the longest x2 40.1 us: shards(): lax.ppermute(lax.dynamic_slice_in_dim(frozen, j * cols, cols, 0), plane,...]
    reduce_scatter x2 -> x0, waiting for transfers between devices: 37.3 us -> none  [the longest x1 37.2 us: shards(): lax.psum_scatter(jnp.dot(frames, projector, preferred_element_type=jnp.fl...]
    all_gather x4, waiting for transfers between devices: 149 us -> 114 us  [the longest x1 67 us: shards(): frame_grad = lax.all_gather(frame_grad, 'fsdp', axis=1, tiled=True)]
    psum x1, blocking collectives: 3.46 us -> 27.2 us  [shards(): lax.psum(jnp.concatenate([jnp.sum(x32 * x32, axis=1), jnp.sum(e32 * e32,...]
    reshape x0 -> x6, local copies, waits for them, and re-layouts: none -> 14.6 us  [the longest x2 10.6 us: shards(): value_part.astype(jnp.bfloat16).reshape(f_size, tok, t_size, v_shard)]
  transfers between devices with their start and end apart: 10 -> 11, of which waited for: 9 -> 6; matrix products, arithmetic and copies ran while one was open for 8% -> 8% of each run, Pallas kernels for 0% -> 0%
where the time goes in v1:
time: 502 us; the launch traced here: 499 us
  waiting for transfers between devices  273 us (54%)
  blocking collectives  71.6 us (14%)
  local copies, waits for them, and re-layouts  58.1 us (12%)
  matrix products  45.5 us (9%)
  starting transfers between devices  18.6 us (4%)
  other arithmetic  18.5 us (4%)
  between operations  14.3 us (3%)
    psum x1, waiting for transfers between devices, shards(): lax.psum(jnp.dot(frames_all, projector_own, preferred_element_type=jnp.fl...  82 us
    all_gather x1, waiting for transfers between devices, shards(): frame_grad = lax.all_gather(frame_grad, 'fsdp', axis=1, tiled=True)  67 us
    ppermute x2, waiting for transfers between devices, shards(): lax.ppermute(lax.dynamic_slice_in_dim(frozen, j * cols, cols, 0), plane,...  40.1 us
    psum x1, waiting for transfers between devices, shards(): down_sum, up_sum = lax.psum((down_part, up_part), 'grp')  35.8 us
    all_gather x1, blocking collectives, shards(): lora_plane = lax.all_gather(lora_tok, 'fsdp', axis=0, tiled=True)  32.5 us
    unnamed x13, local copies, waits for them, and re-layouts  28.2 us
    psum x1, blocking collectives, shards(): lax.psum(jnp.concatenate([jnp.sum(x32 * x32, axis=1), jnp.sum(e32 * e32,...  27.2 us
    all_gather x1, waiting for transfers between devices, shards(): lax.all_gather(jnp.concatenate([down_sum, up_sum.reshape(-1, rank)], axis...  26.3 us
  transfers between devices with their start and end apart: 11, of which 6 were waited for; matrix products, arithmetic and copies ran while one was open for 8% of the time, Pallas kernels for 0%

profile of v1, /device:TPU:0, one launch (start us, length us, event | category | flops | bytes accessed | tf_op | source)
XLA Modules:
  0.0 499.5 jit_solution(9193602135876863072)
XLA Ops:
  9.5 9.7 %all-gather = s32[8,4,4]{2,1,0:T(4,128)S(1)} all-gather(s32[2,4,4]{2,1,0:T(4,128)S(1)} %pad_add_fusion), channel_id=2, replica_groups=mesh['grp'=4,'fsdp'=4,'tp'=2] {'fsdp'}, dimensions={0}, use_global_device_ids=true | all-gather | bytes 640 | tf_op jit(solution)/shard_map/all_gather | solution.py:59
  22.4 2.3 all_gather.30
  25.8 20.9 %all-gather.7.cloned.1.call-done = bf16[768,1280]{1,0:T(8,128)(2,1)} async-done(((bf16[192,1280]{1,0:T(8,128)(2,1)}), bf16[768,1280]{1,0:T(8,128)(2,1)}) %all-gather.7.cloned.1.call-update) | async-done | bytes 1966096 | tf_op jit(solution)/shard_map/all_gather | solution.py:58
  46.7 5.7 %fusion.12 = bf16[768,1024]{0,1:T(8,128)(2,1)} fusion(bf16[768,1280]{1,0:T(8,128)(2,1)} %all-gather.7.cloned.1.call-done, bf16[1280,4096]{1,0:T(8,128)(2,1)} %param.13, s32[]{:T(128)S(6)} %select_n.60), kind=kOutput, calls=%fused_computation.20 | convolution fusion | flops 2014052352 | bytes 6160388 | tf_op jit(solution)/shard_map/dot_general | solution.py:123
  52.5 82.0 %all-reduce.7.cloned.1.call-done = (bf16[768,1024]{0,1:T(8,128)(2,1)}, bf16[192,1024]{1,0:T(8,128)(2,1)}) async-done(((bf16[768,1024]{0,1:T(8,128)(2,1)}, bf16[192,1024]{1,0:T(8,128)(2,1)}), (bf16[768,1024]{0,1:T(8,128)(2,1)}, bf16[192,1024]{1,0:T(8,128)(2,1)})) %all-reduce.7.cloned.1.call-update) | async-done | bytes 1966096 | tf_op jit(solution)/shard_map/psum | solution.py:122
  134.5 3.3 copy.56
  137.8 2.4 copy.57
  140.2 3.6 all-to-all-start
  143.8 3.0 constant_dynamic-slice_fusion
  146.8 9.4 %collective-permute-start = (bf16[1024,512]{1,0:T(8,128)(2,1)}, bf16[1024,512]{1,0:T(8,128)(2,1)}, u32[]{:S(2)}, u32[]{:S(2)}) collective-permute-start(bf16[1024,512]{1,0:T(8,128)(2,1)} %get-tuple-element.30), channel_id=1, source_target_pairs={{0,0},{1,2},{2,4},{3,6},{4,1},{5,3},{6,5},{7,7},{8,8},{9,10},{10,1... | collective-permute-start | bytes 3145736 | tf_op jit(solution)/shard_map/ppermute | solution.py:73
  159.3 2.3 constant_dynamic-update-slice_fusion.1
  161.6 40.1 %collective-permute-done.1 = bf16[1024,512]{1,0:T(8,128)(2,1)} collective-permute-done((bf16[1024,512]{1,0:T(8,128)(2,1)}, bf16[1024,512]{1,0:T(8,128)(2,1)}, u32[]{:S(2)}, u32[]{:S(2)}) %collective-permute-start.1) | collective-permute-done | bytes 1048608 | tf_op jit(solution)/shard_map/ppermute | solution.py:73
  201.7 2.3 constant_dynamic-update-slice_fusion
  204.0 2.6 copy.55
  206.6 4.5 multiply_reduce_fusion
  211.2 4.3 fusion.16
  215.5 6.7 %fusion.2 = (f32[768]{0:T(1024)S(1)}, f32[768]{0:T(1024)S(1)}, f32[768,1024]{0,1:T(8,128)}) fusion(bf16[768,1024]{0,1:T(8,128)(2,1)S(1)} %copy-done.2, f32[1024]{0:T(1024)S(1)} %dynamic_slice.20, f32[768,1024]{0,1:T(8,128)} %fusion.16, bf16[768,1024]{1,0:T(8,128)(2,1)} %all-gather.9.cloned.1.call-done, bf16[1024,1024]{1,0:T(8,128)(2,1)} %constant_dynamic-update-slice_fusion), kind=kOutput, calls=%fused_computation.9 | convolution fusion | flops 1616116224 | bytes 11544576 | tf_op jit(solution)/shard_map/dot_general | solution.py:18
  222.2 27.2 %psum.37 = f32[2560]{0:T(1024)S(1)} all-reduce(f32[2560]{0:T(1024)S(1)} %pad_maximum_fusion.3), channel_id=1, replica_groups=mesh['grp'=4,'fsdp'=4,'tp'=2] {'fsdp','tp'}, use_global_device_ids=true, to_apply=%region_12.13 | all-reduce | flops 2560 | bytes 20480 | tf_op jit(solution)/shard_map/psum | solution.py:135
  249.3 2.6 fusion.1
  253.5 5.3 %add_convert_fusion = bf16[1024,1024]{1,0:T(8,128)(2,1)} fusion(f32[1024,1024]{1,0:T(8,128)S(1)} %fusion.23, bf16[1024,1024]{1,0:T(8,128)(2,1)S(1)} %fusion.1, bf16[1024,1024]{1,0:T(8,128)(2,1)} %constant_dynamic-update-slice_fusion), kind=kOutput, calls=%fused_computation.7 | convolution fusion | flops 2150629376 | bytes 10485760 | tf_op jit(solution)/shard_map/dot_general | solution.py:158
  258.7 4.5 reshape.66
  263.2 6.1 %copy.61 = bf16[4,256,2,512]{1,3,2,0:T(8,128)(2,1)} copy(bf16[4,256,2,512]{3,2,1,0:T(2,128)(2,1)} %reshape.66) | data formatting | bytes 4194304 | tf_op jit(solution)/shard_map/reshape | solution.py:162
  269.4 3.2 pad_maximum_fusion
  272.5 4.4 all-to-all-start.1
  277.2 32.5 %all_gather.33 = bf16[1024,64]{0,1:T(8,128)(2,1)S(1)} all-gather(bf16[256,64]{0,1:T(8,128)(2,1)S(1)} %fusion.17), channel_id=1, replica_groups=mesh['grp'=4,'fsdp'=4,'tp'=2] {'fsdp'}, dimensions={0}, use_global_device_ids=true | all-gather | bytes 163840 | tf_op jit(solution)/shard_map/all_gather | solution.py:115
  314.3 35.8 %all-reduce.5.cloned.1.call-done = (f32[512,64]{0,1:T(8,128)}, f32[1024,64]{0,1:T(8,128)}) async-done(((f32[512,64]{0,1:T(8,128)}, f32[1024,64]{0,1:T(8,128)}), (f32[512,64]{0,1:T(8,128)}, f32[1024,64]{0,1:T(8,128)})) %all-reduce.5.cloned.1.call-update) | async-done | bytes 393232 | tf_op jit(solution)/shard_map/psum | solution.py:178
  352.2 3.6 fusion.6
  356.7 26.3 %all-gather.13.cloned.1.call-done = f32[6144,64]{0,1:T(8,128)} async-done(((f32[1536,64]{0,1:T(8,128)}), f32[6144,64]{0,1:T(8,128)}) %all-gather.13.cloned.1.call-update) | async-done | bytes 1572880 | tf_op jit(solution)/shard_map/all_gather | solution.py:179
  383.0 2.4 reshape.73
  388.3 67.0 %all-gather.11.cloned.1.call-done = bf16[768,4096]{0,1:T(8,128)(2,1)} async-done(((bf16[768,1024]{0,1:T(8,128)(2,1)}), bf16[768,4096]{0,1:T(8,128)(2,1)}) %all-gather.11.cloned.1.call-update) | async-done | bytes 6291472 | tf_op jit(solution)/shard_map/all_gather | solution.py:153
  455.3 14.9 %convolution_bitcast_fusion = f32[1280,4096]{0,1:T(8,128)} fusion(bf16[768,4096]{0,1:T(8,128)(2,1)} %all-gather.11.cloned.1.call-done, bf16[768,1280]{1,0:T(8,128)(2,1)} %all-gather.7.cloned.1.call-done), kind=kOutput, calls=%fused_computation | convolution fusion | flops 8053063680 | bytes 29229056 | tf_op jit(solution)/shard_map/dot_general | solution.py:12
  470.2 22.4 %copy.65 = f32[1280,4096]{1,0:T(8,128)} copy(f32[1280,4096]{0,1:T(8,128)} %convolution_bitcast_fusion) | data formatting | bytes 41943040
  (70 shorter events, 21.9 us)
Async XLA Ops:
  7.2 149.1 %copy-start = (bf16[2048,64]{0,1:T(8,128)(2,1)S(1)}, bf16[2048,64]{0,1:T(8,128)(2,1)}, u32[]{:S(2)}) copy-start(bf16[2048,64]{0,1:T(8,128)(2,1)} %param.17) | copy-start | bytes 786436
  7.2 39.5 %all-gather.7.cloned.1.call-start = ((), (), s32[]{:S(2)}) async-start(), calls=%async_computation.2 | async-start | bytes 2457600 | tf_op jit(solution)/shard_map/all_gather | solution.py:58
  7.9 126.6 %all-reduce.7.cloned.1.call-start = ((), (), s32[]{:S(2)}) async-start(), calls=%async_computation.7 | async-start | bytes 3932160 | tf_op jit(solution)/shard_map/psum | solution.py:122
  52.5 158.7 %all-gather.9.cloned.1.call-start = ((), (), s32[]{:S(2)}) async-start(), calls=%async_computation.3 | async-start | bytes 1966080 | tf_op jit(solution)/shard_map/all_gather | solution.py:117
  140.2 66.4 %all-to-all-start = ((bf16[4,256,1024]{2,1,0:T(8,128)(2,1)}), bf16[4,256,1024]{2,1,0:T(8,128)(2,1)S(1)}, u32[]{:S(2)}, u32[]{:S(2)}) async-start(bf16[4,256,1024]{2,1,0:T(8,128)(2,1)} %bitcast.60), calls=%async_computation | async-start | bytes 4194304 | tf_op jit(solution)/shard_map/all_to_all | solution.py:60
  146.8 10.9 %collective-permute-start = (bf16[1024,512]{1,0:T(8,128)(2,1)}, bf16[1024,512]{1,0:T(8,128)(2,1)}, u32[]{:S(2)}, u32[]{:S(2)}) collective-permute-start(bf16[1024,512]{1,0:T(8,128)(2,1)} %get-tuple-element.30), channel_id=1, source_target_pairs={{0,0},{1,2},{2,4},{3,6},{4,1},{5,3},{6,5},{7,7},{8,8},{9,10},{10,1... | collective-permute-start | bytes 3145736 | tf_op jit(solution)/shard_map/ppermute | solution.py:73
  156.3 45.4 %collective-permute-start.1 = (bf16[1024,512]{1,0:T(8,128)(2,1)}, bf16[1024,512]{1,0:T(8,128)(2,1)}, u32[]{:S(2)}, u32[]{:S(2)}) collective-permute-start(bf16[1024,512]{1,0:T(8,128)(2,1)} %get-tuple-element.29), channel_id=1, source_target_pairs={{0,2},{1,0},{2,6},{3,4},{4,3},{5,1},{6,7},{7,5},{8,10},{9,8},{10,1... | collective-permute-start | bytes 3145736 | tf_op jit(solution)/shard_map/ppermute | solution.py:73
  156.3 54.8 %collective-permute-start.2 = (bf16[1024,64]{0,1:T(8,128)(2,1)S(1)}, bf16[1024,64]{0,1:T(8,128)(2,1)S(1)}, u32[]{:S(2)}, u32[]{:S(2)}) collective-permute-start(bf16[1024,64]{0,1:T(8,128)(2,1)S(1)} %constant_dynamic-slice_fusion.2), channel_id=1, source_target_pairs={{0,0},{1,2},{2,4},{3,6},{4,1},{5,3},{6,5},{7,7},{8,8},{9,10},{10,1... | collective-permute-start | bytes 393224 | tf_op jit(solution)/shard_map/ppermute | solution.py:80
  211.1 4.3 copy-start.2
  272.5 38.4 %all-to-all-start.1 = ((bf16[8,256,576]{1,2,0:T(8,128)(2,1)}), bf16[8,256,576]{1,2,0:T(8,128)(2,1)}, u32[]{:S(2)}, u32[]{:S(2)}) async-start(bf16[8,256,576]{1,2,0:T(8,128)(2,1)} %bitcast.59), calls=%async_computation.1 | async-start | bytes 4718592 | tf_op jit(solution)/shard_map/all_to_all | solution.py:171
  276.9 73.2 %all-reduce.5.cloned.1.call-start = ((), (), s32[]{:S(2)}) async-start(), calls=%async_computation.6 | async-start | bytes 786432 | tf_op jit(solution)/shard_map/psum | solution.py:178
  310.9 41.2 %copy-start.3 = (bf16[768,1024]{0,1:T(8,128)(2,1)S(1)}, bf16[768,1024]{0,1:T(8,128)(2,1)}, u32[]{:S(2)}) copy-start(bf16[768,1024]{0,1:T(8,128)(2,1)} %get-tuple-element.27) | copy-start | bytes 4718596
  314.3 68.8 %all-gather.13.cloned.1.call-start = ((), (), s32[]{:S(2)}) async-start(), calls=%async_computation.5 | async-start | bytes 1966080 | tf_op jit(solution)/shard_map/all_gather | solution.py:179
  351.9 103.4 %all-gather.11.cloned.1.call-start = ((), (), s32[]{:S(2)}) async-start(), calls=%async_computation.4 | async-start | bytes 7864320 | tf_op jit(solution)/shard_map/all_gather | solution.py:153
  470.2 22.4 %copy-start.1 = (bf16[2048,64]{0,1:T(8,128)(2,1)S(1)}, bf16[2048,64]{0,1:T(8,128)(2,1)}, u32[]{:S(2)}) copy-start(bf16[2048,64]{0,1:T(8,128)(2,1)} %param.17) | copy-start | bytes 786436
Sparse Core Ops, SparseCore 0:
  9.8 36.8 all-gather.6
  52.6 81.8 all-reduce.6
  136.3 52.9 all-gather.8
  314.4 35.6 all-reduce.4
  352.3 30.6 all-gather.12
  385.3 70.0 all-gather.10

commit v2 on v1

--- a/solution.py
+++ b/solution.py
@@ -1,11 +1,337 @@
+import functools
+import math
+
 import jax
 import jax.numpy as jnp
 from jax import lax
+from jax.experimental import pallas as pl
+from jax.experimental.pallas import tpu as pltpu
 from jax.sharding import PartitionSpec as P
 
 adapter_scale = 2.0
 norm_eps = 1e-05
 plane = ("fsdp", "tp")
+
+MESH = pl.DeviceIdType.MESH
+VMEM = pl.BlockSpec(memory_space=pltpu.VMEM)
+DMA = pltpu.SemaphoreType.DMA
+VMEM_LIMIT = 48 * 1024 * 1024
+
+
+def push(src, dst, send_sem, recv_sem, device_id):
+    return pltpu.make_async_remote_copy(
+        src_ref=src,
+        dst_ref=dst,
+        send_sem=send_sem,
+        recv_sem=recv_sem,
+        device_id=device_id,
+        device_id_type=MESH,
+    )
+
+
+def greet_plane(f_size, t_size):
+    me = lax.axis_index("fsdp") * t_size + lax.axis_index("tp")
+    barrier = pltpu.get_barrier_semaphore()
+    for k in range(1, f_size * t_size):
+        p = lax.rem(me + k, f_size * t_size)
+        where = {"fsdp": lax.div(p, t_size), "tp": lax.rem(p, t_size)}
+        pl.semaphore_signal(barrier, inc=1, device_id=where, device_id_type=MESH)
+    pl.semaphore_wait(barrier, f_size * t_size - 1)
+
+
+def exchange_kernel(
+    f_size,
+    t_size,
+    frames_ref,
+    text_ref,
+    frozen_ref,
+    frames_out,
+    text_out,
+    frozen_out,
+    send_a,
+    recv_a,
+    send_b,
+    recv_b,
+    send_w,
+    recv_w,
+    local,
+):
+    f, t = lax.axis_index("fsdp"), lax.axis_index("tp")
+    rows = frames_ref.shape[0]
+    tok = text_ref.shape[0]
+    cols = text_out.shape[1]
+    v = frozen_ref.shape[1]
+    greet_plane(f_size, t_size)
+
+    def columns(i, size):
+        return pl.ds(pl.multiple_of(i * size, 128), size)
+
+    copies = []
+    for k in range(1, f_size):
+        p = lax.rem(f + k, f_size)
+        copies.append(
+            push(
+                frames_ref,
+                frames_out.at[pl.ds(f * rows, rows)],
+                send_a.at[k - 1],
+                recv_a.at[k - 1],
+                {"fsdp": p},
+            )
+        )
+    for k in range(1, f_size):
+        p = lax.rem(f + k, f_size)
+        copies.append(
+            push(
+                text_ref.at[:, columns(p, cols)],
+                text_out.at[pl.ds(f * tok, tok)],
+                send_b.at[k - 1],
+                recv_b.at[k - 1],
+                {"fsdp": p},
+            )
+        )
+    for c in copies:
+        c.start()
+    own = [
+        pltpu.make_async_copy(frames_ref, frames_out.at[pl.ds(f * rows, rows)], local.at[0]),
+        pltpu.make_async_copy(
+            text_ref.at[:, columns(f, cols)], text_out.at[pl.ds(f * tok, tok)], local.at[1]
+        ),
+    ]
+    for c in own:
+        c.start()
+    weights = []
+    for j in range(t_size):
+        b = f * t_size + j
+        d_f, d_t = lax.rem(b, f_size), lax.div(b, f_size)
+        mine = jnp.logical_and(d_f == f, d_t == t)
+        src = frozen_ref.at[pl.ds(j * cols, cols)]
+        dst = frozen_out.at[:, columns(t, v)]
+        far = push(src, dst, send_w.at[j], recv_w.at[t], {"fsdp": d_f, "tp": d_t})
+        near = pltpu.make_async_copy(src, dst, local.at[2])
+        weights.append((mine, far, near))
+        pl.when(jnp.logical_not(mine))(far.start)
+        pl.when(mine)(near.start)
+    for c in own:
+        c.wait()
+    for c in copies:
+        c.wait_recv()
+        c.wait_send()
+    for mine, far, near in weights:
+        pl.when(jnp.logical_not(mine))(far.wait_send)
+        pl.when(mine)(near.wait)
+    source = lax.div(t * f_size + f, t_size)
+    for ts in range(t_size):
+        arrive = push(
+            frozen_ref.at[pl.ds(0, cols)],
+            frozen_out.at[:, pl.ds(ts * v, v)],
+            send_w.at[0],
+            recv_w.at[ts],
+            {"fsdp": lax.rem(f + 1, f_size)},
+        )
+        pl.when(jnp.logical_not(jnp.logical_and(source == f, t == ts)))(arrive.wait_recv)
+
+
+def exchange(frames, text, frozen, f_size, t_size):
+    cols = text.shape[1] // f_size
+    return pl.pallas_call(
+        functools.partial(exchange_kernel, f_size, t_size),
+        out_shape=(
+            jax.ShapeDtypeStruct((frames.shape[0] * f_size, frames.shape[1]), frames.dtype),
+            jax.ShapeDtypeStruct((text.shape[0] * f_size, cols), text.dtype),
+            jax.ShapeDtypeStruct((cols, frozen.shape[1] * t_size), frozen.dtype),
+        ),
+        in_specs=[VMEM] * 3,
+        out_specs=(VMEM,) * 3,
+        scratch_shapes=[DMA((f_size - 1,))] * 4 + [DMA((t_size,))] * 2 + [DMA((3,))],
+        compiler_params=pltpu.CompilerParams(
+            collective_id=0, has_side_effects=True, vmem_limit_bytes=VMEM_LIMIT
+        ),
+        name="exchange",
+    )(frames, text, frozen)
+
+
+def line_kernel(n, chunks, x_ref, o_ref, from_left, from_right, to_right, to_left, *sems):
+    send_r, recv_r, send_l, recv_l = sems
+    g = lax.axis_index("grp")
+    rows = x_ref.shape[0] // chunks
+    right, left = jnp.minimum(g + 1, n - 1), jnp.maximum(g - 1, 0)
+    has_left, has_right = g > 0, g < n - 1
+    barrier = pltpu.get_barrier_semaphore()
+
+    @pl.when(has_left)
+    def _():
+        pl.semaphore_signal(barrier, inc=1, device_id={"grp": left}, device_id_type=MESH)
+
+    @pl.when(has_right)
+    def _():
+        pl.semaphore_signal(barrier, inc=1, device_id={"grp": right}, device_id_type=MESH)
+
+    pl.semaphore_wait(barrier, has_left.astype(jnp.int32) + has_right.astype(jnp.int32))
+
+    def part(c):
+        return pl.ds(pl.multiple_of(c * rows, rows), rows)
+
+    def rightward(c):
+        return push(
+            to_right.at[part(c)], from_left.at[part(c)], send_r.at[c], recv_r.at[c], {"grp": right}
+        )
+
+    def leftward(c):
+        return push(
+            to_left.at[part(c)], from_right.at[part(c)], send_l.at[c], recv_l.at[c], {"grp": left}
+        )
+
+    def step(c, has_in, has_out, copy, came, going):
+        fits = jnp.logical_and(c >= 0, c < chunks)
+
+        @pl.when(jnp.logical_and(fits, has_in))
+        def _():
+            copy(c).wait_recv()
+
+        @pl.when(jnp.logical_and(fits, jnp.logical_and(has_in, has_out)))
+        def _():
+            total = came[part(c)].astype(jnp.float32) + x_ref[part(c)].astype(jnp.float32)
+            going[part(c)] = total.astype(going.dtype)
+            copy(c).start()
+
+        @pl.when(jnp.logical_and(fits, jnp.logical_and(jnp.logical_not(has_in), has_out)))
+        def _():
+            going[part(c)] = x_ref[part(c)]
+            copy(c).start()
+
+    def body(i, carry):
+        step(i - g, has_left, has_right, rightward, from_left, to_right)
+        step(i - (n - 1 - g), has_right, has_left, leftward, from_right, to_left)
+        return carry
+
+    lax.fori_loop(0, chunks + n - 1, body, 0)
+
+    def finish(c, carry):
+        @pl.when(jnp.logical_not(has_left))
+        def _():
+            total = x_ref[part(c)].astype(jnp.float32) + from_right[part(c)].astype(jnp.float32)
+            o_ref[part(c)] = total.astype(o_ref.dtype)
+
+        @pl.when(jnp.logical_not(has_right))
+        def _():
+            total = x_ref[part(c)].astype(jnp.float32) + from_left[part(c)].astype(jnp.float32)
+            o_ref[part(c)] = total.astype(o_ref.dtype)
+
+        @pl.when(jnp.logical_and(has_left, has_right))
+        def _():
+            total = from_left[part(c)].astype(jnp.float32) + from_right[part(c)].astype(jnp.float32)
+            total = total + x_ref[part(c)].astype(jnp.float32)
+            o_ref[part(c)] = total.astype(o_ref.dtype)
+
+        @pl.when(has_right)
+        def _():
+            rightward(c).wait_send()
+
+        @pl.when(has_left)
+        def _():
+            leftward(c).wait_send()
+
+        return carry
+
+    lax.fori_loop(0, chunks, finish, 0)
+
+
+def line_sum(x, n, chunks, collective_id):
+    return pl.pallas_call(
+        functools.partial(line_kernel, n, chunks),
+        out_shape=jax.ShapeDtypeStruct(x.shape, x.dtype),
+        in_specs=[VMEM],
+        out_specs=VMEM,
+        scratch_shapes=[pltpu.VMEM(x.shape, x.dtype)] * 4 + [DMA((chunks,))] * 4,
+        compiler_params=pltpu.CompilerParams(
+            collective_id=collective_id, has_side_effects=True, vmem_limit_bytes=VMEM_LIMIT
+        ),
+        name="line_sum",
+    )(x)
+
+
+def plane_sum_kernel(f_size, t_size, x_ref, o_ref, slots, send, recv):
+    count = f_size * t_size
+    me = lax.axis_index("fsdp") * t_size + lax.axis_index("tp")
+    greet_plane(f_size, t_size)
+    copies = []
+    for k in range(1, count):
+        p = lax.rem(me + k, count)
+        where = {"fsdp": lax.div(p, t_size), "tp": lax.rem(p, t_size)}
+        copies.append(push(x_ref, slots.at[k - 1], send.at[k - 1], recv.at[k - 1], where))
+        copies[-1].start()
+    total = x_ref[...]
+    for k in range(1, count):
+        copies[k - 1].wait_recv()
+        total = total + slots[k - 1]
+    o_ref[...] = total
+    for c in copies:
+        c.wait_send()
+
+
+def plane_sum(x, f_size, t_size):
+    count = f_size * t_size - 1
+    return pl.pallas_call(
+        functools.partial(plane_sum_kernel, f_size, t_size),
+        out_shape=jax.ShapeDtypeStruct(x.shape, x.dtype),
+        in_specs=[VMEM],
+        out_specs=VMEM,
+        scratch_shapes=[pltpu.VMEM((count,) + x.shape, x.dtype), DMA((count,)), DMA((count,))],
+        compiler_params=pltpu.CompilerParams(collective_id=2, has_side_effects=True),
+        name="plane_sum",
+    )(x)
+
+
+def gather_kernel(f_size, x_ref, o_ref, send, recv):
+    f = lax.axis_index("fsdp")
+    barrier = pltpu.get_barrier_semaphore()
+    for k in range(1, f_size):
+        where = {"fsdp": lax.rem(f + k, f_size)}
+        pl.semaphore_signal(barrier, inc=1, device_id=where, device_id_type=MESH)
+    pl.semaphore_wait(barrier, f_size - 1)
+    copies = []
+    for k in range(1, f_size):
+        where = {"fsdp": lax.rem(f + k, f_size)}
+        copies.append(push(x_ref, o_ref.at[f], send.at[k - 1], recv.at[k - 1], where))
+        copies[-1].start()
+    o_ref[f] = x_ref[...]
+    for c in copies:
+        c.wait_recv()
+        c.wait_send()
+
+
+def fsdp_gather(x, f_size, collective_id):
+    return pl.pallas_call(
+        functools.partial(gather_kernel, f_size),
+        out_shape=jax.ShapeDtypeStruct((f_size,) + x.shape, x.dtype),
+        in_specs=[VMEM],
+        out_specs=VMEM,
+        scratch_shapes=[DMA((f_size - 1,)), DMA((f_size - 1,))],
+        compiler_params=pltpu.CompilerParams(collective_id=collective_id, has_side_effects=True),
+        name="fsdp_gather",
+    )(x)
+
+
+def product_kernel(a_ref, b_ref, o_ref):
+    o_ref[...] = jnp.dot(a_ref[...], b_ref[...], preferred_element_type=jnp.float32)
+
+
+def product(a, b):
+    m, k = a.shape
+    n = b.shape[1]
+    bm, bn = math.gcd(m, 256), math.gcd(n, 1024)
+    return pl.pallas_call(
+        product_kernel,
+        out_shape=jax.ShapeDtypeStruct((m, n), jnp.float32),
+        grid=(n // bn, m // bm),
+        in_specs=[
+            pl.BlockSpec((bm, k), lambda j, i: (i, 0)),
+            pl.BlockSpec((k, bn), lambda j, i: (0, j)),
+        ],
+        out_specs=pl.BlockSpec((bm, bn), lambda j, i: (i, j)),
+        compiler_params=pltpu.CompilerParams(vmem_limit_bytes=VMEM_LIMIT),
+        name="product",
+    )(a, b)
 
 
 def contract_leading(left_side, right_side):
@@ -55,28 +381,7 @@
     v_full = v_shard * t_size
     rank = adapter_down_map.shape[1]
 
-    frames_all = lax.all_gather(frames, "fsdp", axis=0, tiled=True)
     clips = lax.all_gather(jnp.stack([clip_frame_length[0], audio_first_token[0]]), "fsdp", axis=0)
-    text = lax.all_to_all(
-        text_token_embedding.reshape(tok, f_size, cols).transpose(1, 0, 2),
-        "fsdp",
-        split_axis=0,
-        concat_axis=0,
-        tiled=True,
-    )
-
-    own_block = t_idx * f_size + f_idx
-    own_j = lax.rem(own_block, t_size)
-    frozen_own = jnp.zeros((cols, v_full), jnp.bfloat16)
-    for shift in range(t_size):
-        j = lax.rem(t_idx + shift, t_size)
-        piece = lax.ppermute(
-            lax.dynamic_slice_in_dim(frozen, j * cols, cols, 0),
-            plane,
-            block_perm(f_size, t_size, shift),
-        )
-        t_src = lax.rem(own_j - shift + t_size, t_size)
-        frozen_own = lax.dynamic_update_slice_in_dim(frozen_own, piece, t_src * v_shard, 1)
     down_own = lax.ppermute(
         lax.dynamic_slice_in_dim(adapter_down_map, t_idx * cols, cols, 0),
         plane,
@@ -114,14 +419,20 @@
     lora_tok = (adapter_scale * contract_trailing(grad_full, up_full)).astype(jnp.bfloat16)
     lora_plane = lax.all_gather(lora_tok, "fsdp", axis=0, tiled=True)
     grad_rows = lax.psum(contract_leading(take_own, grad_full).astype(jnp.bfloat16), "grp")
+
+    frames_all, text, frozen_own = exchange(frames, text_token_embedding, frozen, f_size, t_size)
+    text = text.reshape(f_size, tok, cols)
+    grad_rows, frames_all = lax.optimization_barrier((grad_rows, frames_all))
     grad_rows = lax.all_gather(grad_rows, "fsdp", axis=0, tiled=True)
     lora_rows = (adapter_scale * contract_trailing(grad_rows, up_full)).astype(jnp.bfloat16)
     grad_norm = contract_trailing(grad_rows, frozen_own) + contract_trailing(lora_rows, down_own)
 
     projector_own = lax.dynamic_slice_in_dim(projector, f_idx * cols, cols, 1)
-    embedded = lax.psum(
+    embedded = line_sum(
         jnp.dot(frames_all, projector_own, preferred_element_type=jnp.float32).astype(jnp.bfloat16),
-        "grp",
+        lax.axis_size("grp"),
+        16,
+        1,
     )
     audio = lax.dot_general(
         take,
@@ -132,26 +443,25 @@
     x = jnp.where(is_audio[:, :, None], audio, text).reshape(f_size * tok, cols)
     x32 = x.astype(jnp.float32)
     e32 = embedded.astype(jnp.float32)
-    stats = lax.psum(
-        jnp.concatenate(
-            [
-                jnp.sum(x32 * x32, axis=1),
-                jnp.sum(e32 * e32, axis=1),
-                jnp.sum(e32 * gain_own[None, :] * grad_norm, axis=1),
-            ]
-        ),
-        plane,
-    )
+    stats = jnp.concatenate(
+        [
+            jnp.sum(x32 * x32, axis=1),
+            jnp.sum(e32 * e32, axis=1),
+            jnp.sum(e32 * gain_own[None, :] * grad_norm, axis=1),
+        ]
+    )
+    stats = jnp.pad(stats, (0, -stats.shape[0] % 1024)).reshape(-1, 128)
+    stats = plane_sum(stats, f_size, t_size).reshape(-1)
     n_tok, n_frames = f_size * tok, f_size * block_frames
     inv_tok = lax.rsqrt(stats[:n_tok] / full_width + norm_eps)
     inv_frame = lax.rsqrt(stats[n_tok : n_tok + n_frames] / full_width + norm_eps)
-    dots = inv_frame * stats[n_tok + n_frames :]
+    dots = inv_frame * stats[n_tok + n_frames : n_tok + 2 * n_frames]
     frame_grad = (
         (inv_frame[:, None] * gain_own[None, :]) * grad_norm
         - e32 * (inv_frame * inv_frame * dots / full_width)[:, None]
     ).astype(jnp.bfloat16)
     frame_grad = lax.all_gather(frame_grad, "fsdp", axis=1, tiled=True)
-    projector_grad = contract_leading(frames_all, frame_grad)
+    projector_grad = product(frames_all.T, frame_grad)
 
     normed = (x32 * inv_tok[:, None] * gain_own[None, :]).astype(jnp.bfloat16)
     low_part = jnp.dot(normed, down_own, preferred_element_type=jnp.float32)
@@ -175,12 +485,12 @@
 
     up_part = adapter_scale * contract_leading(low_half, grad_out)
     down_part = contract_leading(normed, lora_plane)
-    down_sum, up_sum = lax.psum((down_part, up_part), "grp")
-    gathered = lax.all_gather(
-        jnp.concatenate([down_sum, up_sum.reshape(-1, rank)], axis=0), "fsdp", axis=0
-    )
-    down_map_gradient = gathered[:, :cols].reshape(width, rank)
-    up_map_gradient = jnp.sum(gathered[:, cols:], axis=0).reshape(rank, v_shard)
+    both_parts = jnp.concatenate([down_part.reshape(-1, 128), up_part.reshape(-1, 128)], axis=0)
+    summed = line_sum(both_parts, lax.axis_size("grp"), 4, 3)
+    gathered = fsdp_gather(summed, f_size, 4)
+    split = cols * rank // 128
+    down_map_gradient = gathered[:, :split].reshape(width, rank)
+    up_map_gradient = jnp.sum(gathered[:, split:], axis=0).reshape(rank, v_shard)
     return (value_output, projector_grad, down_map_gradient, up_map_gradient)
 
 

time: 502 us -> 353 us (0.70)
  waiting for transfers between devices: 273 us -> 0.06 us
  Pallas kernels: 0 us -> 211 us
  local copies, waits for them, and re-layouts: 58.1 us -> 23.3 us
  matrix products: 45.5 us -> 25.8 us
  blocking collectives: 71.6 us -> 55.1 us
  starting transfers between devices: 18.6 us -> 5.17 us
    pallas_call x0 -> x6, Pallas kernels: none -> 211 us  [the longest x2 89.8 us: line_sum(): pl.pallas_call(functools.partial(line_kernel, n, chunks), out_shape=jax.S...]
    psum x2 -> x1, waiting for transfers between devices: 118 us -> 0.01 us  [shards(): lax.psum(contract_leading(take_own, grad_full).astype(jnp.bfloat16), 'grp')]
    all_gather x1, waiting for transfers between devices: 67 us -> 0.01 us  [shards(): frame_grad = lax.all_gather(frame_grad, 'fsdp', axis=1, tiled=True)]
    all_gather x2 -> x0, waiting for transfers between devices: 47.2 us -> none  [the longest x1 26.3 us: shards(): lax.all_gather(jnp.concatenate([down_sum, up_sum.reshape(-1, rank)], axis...]
    ppermute x2 -> x0, waiting for transfers between devices: 40.1 us -> none  [shards(): lax.ppermute(lax.dynamic_slice_in_dim(frozen, j * cols, cols, 0), plane,...]
    psum x1 -> x0, blocking collectives: 27.2 us -> none  [shards(): lax.psum(jnp.concatenate([jnp.sum(x32 * x32, axis=1), jnp.sum(e32 * e32,...]
    unnamed x13 -> x27, local copies, waits for them, and re-layouts: 28.2 us -> 9.91 us
    dot_general x4 -> x3, matrix products: 17.2 us -> 3.51 us  [contract_leading(): lax.dot_general(left_side, right_side, (((0,), (0,)), ((), ())), preferre...]
  transfers between devices with their start and end apart: 11 -> 5, of which waited for: 6 -> 0; matrix products, arithmetic and copies ran while one was open for 8% -> 12% of each run, Pallas kernels for 0% -> 51%
where the time goes in v2:
time: 353 us; the launch traced here: 352 us
  Pallas kernels  211 us (60%)
  blocking collectives  55.1 us (16%)
  matrix products  25.8 us (7%)
  local copies, waits for them, and re-layouts  23.3 us (7%)
  other arithmetic  17.6 us (5%)
  between operations  14.1 us (4%)
  starting transfers between devices  5.17 us (1%)
    pallas_call x2, Pallas kernels, line_sum(): pl.pallas_call(functools.partial(line_kernel, n, chunks), out_shape=jax.S...  89.8 us
    pallas_call x1, Pallas kernels, exchange(): pl.pallas_call(functools.partial(exchange_kernel, f_size, t_size), out_sh...  71.8 us
    all_gather x1, blocking collectives, shards(): lora_plane = lax.all_gather(lora_tok, 'fsdp', axis=0, tiled=True)  43.1 us
    pallas_call x1, Pallas kernels, product(): pl.pallas_call(product_kernel, out_shape=jax.ShapeDtypeStruct((m, n), jnp...  19.6 us
    pallas_call x1, Pallas kernels, fsdp_gather(): pl.pallas_call(functools.partial(gather_kernel, f_size), out_shape=jax.Sh...  17.4 us
    pallas_call x1, Pallas kernels, plane_sum(): pl.pallas_call(functools.partial(plane_sum_kernel, f_size, t_size), out_s...  12.4 us
    dot_general x3, matrix products, contract_trailing(): lax.dot_general(left_side, right_side, (((1,), (1,)), ((), ())), preferre...  11.4 us
    unnamed x27, local copies, waits for them, and re-layouts  9.91 us
  transfers between devices with their start and end apart: 5, of which 0 were waited for; matrix products, arithmetic and copies ran while one was open for 12% of the time, Pallas kernels for 51%

profile of v2, /device:TPU:0, one launch (start us, length us, event | category | flops | bytes accessed | tf_op | source)
XLA Modules:
  0.0 352.1 jit_solution(2586403271873760155)
XLA Ops:
  7.3 0.9 select_reduce_fusion
  8.9 9.7 %all-gather = s32[8,4,4]{2,1,0:T(4,128)S(1)} all-gather(s32[2,4,4]{2,1,0:T(4,128)S(1)} %pad_add_fusion), channel_id=2, replica_groups=mesh['grp'=4,'fsdp'=4,'tp'=2] {'fsdp'}, dimensions={0}, use_global_device_ids=true | all-gather | bytes 640 | tf_op jit(solution)/shard_map/all_gather | solution.py:384
  19.9 1.1 broadcast_multiply_fusion
  21.6 0.9 pad_maximum_fusion.2
  22.5 2.3 all_gather.20
  24.8 1.0 convolution_convert_fusion
  25.9 71.8 %exchange.1 = (bf16[768,1280]{1,0:T(8,128)(2,1)S(1)}, bf16[1024,1024]{1,0:T(8,128)(2,1)S(1)}, bf16[1024,1024]{1,0:T(8,128)(2,1)}) custom-call(bf16[192,1280]{1,0:T(8,128)(2,1)S(1)} %copy-done.6, bf16[256,4096]{1,0:T(8,128)(2,1)} %text_ref.1, bf16[2048,512]{1,0:T(8,128)(2,1)} %frozen_ref.1), custom_call_target="tpu_custom_call" | custom-call | tf_op jit(solution)/shard_map/exchange/pallas_call | solution.py:136
  97.7 1.3 copy-done.2
  100.5 3.9 %fusion.9.x_ref = bf16[768,1024]{1,0:T(8,128)(2,1)S(1)} fusion(bf16[768,1280]{1,0:T(8,128)(2,1)S(1)} %get-tuple-element.10, bf16[1280,4096]{1,0:T(8,128)(2,1)} %param.13, s32[]{:T(128)S(6)} %select_n.50), kind=kOutput, calls=%fused_computation.18 | convolution fusion | flops 2014052352 | bytes 6160388 | tf_op jit(solution)/shard_map/dot_general | solution.py:432
  104.5 64.7 %line_sum.2 = bf16[768,1024]{1,0:T(8,128)(2,1)S(1)} custom-call(bf16[768,1024]{1,0:T(8,128)(2,1)S(1)} %fusion.9.x_ref), custom_call_target="tpu_custom_call" | custom-call | tf_op jit(solution)/shard_map/line_sum/pallas_call | solution.py:240
  169.2 3.1 multiply_reduce_fusion
  172.3 5.6 %fusion.38 = f32[768,1024]{1,0:T(8,128)} fusion(bf16[768,1024]{1,0:T(8,128)(2,1)} %all-gather.4.cloned.1.call-done, bf16[1024,1024]{1,0:T(8,128)(2,1)} %get-tuple-element.13), kind=kOutput, calls=%fused_computation.73 | convolution fusion | flops 1610612736 | bytes 6815744 | tf_op jit(solution)/shard_map/dot_general | solution.py:344
  177.9 5.6 %fusion.2 = (f32[768]{0:T(1024)S(1)}, f32[768]{0:T(1024)S(1)}, f32[768,1024]{1,0:T(8,128)}) fusion(bf16[768,1024]{1,0:T(8,128)(2,1)S(1)} %line_sum.2, f32[1024]{0:T(1024)S(1)} %dynamic_slice.15, f32[768,1024]{1,0:T(8,128)} %fusion.38, bf16[1024,64]{0,1:T(8,128)(2,1)S(1)} %collective-permute-done, bf16[768,1024]{1,0:T(8,128)(2,1)} %all-gather.4.cloned.1.call-done, ...), kind=kOutput, calls=%fused_computation.8 | convolution fusion | flops 206928384 | bytes 9709568 | tf_op jit(solution)/shard_map/dot_general | solution.py:344
  184.1 12.4 %plane_sum.1 = f32[24,128]{1,0:T(8,128)} custom-call(f32[24,128]{1,0:T(8,128)} %fusion.27.x_ref), custom_call_target="tpu_custom_call" | custom-call | tf_op jit(solution)/shard_map/plane_sum/pallas_call | solution.py:274
  197.9 3.7 %fusion.6 = bf16[768,1024]{1,0:T(8,128)(2,1)} fusion(bf16[768,1024]{1,0:T(8,128)(2,1)S(1)} %line_sum.2, f32[768,1024]{1,0:T(8,128)} %get-tuple-element.37, f32[768]{0:T(1024)S(1)} %fusion.30, f32[768]{0:T(1024)S(1)} %rsqrt_bitcast_fusion, f32[1024]{0:T(1024)S(1)} %dynamic_slice.15), kind=kLoop, calls=%fused_computation.12 | loop fusion | flops 4718592 | bytes 6301696 | tf_op jit(solution)/shard_map/convert_element_type | solution.py:462
  202.3 2.6 fusion.1
  205.8 1.7 copy-done.11
  207.5 2.3 fusion.39
  210.6 2.8 reshape.109
  213.3 4.7 %copy.46 = bf16[4,256,2,512]{1,3,2,0:T(8,128)(2,1)S(1)} copy(bf16[4,256,2,512]{3,2,1,0:T(2,128)(2,1)} %reshape.109) | data formatting | bytes 4194304 | tf_op jit(solution)/shard_map/reshape | solution.py:472
  218.1 1.6 pad_maximum_fusion
  219.6 4.4 %all-to-all-start = ((bf16[8,256,576]{1,2,0:T(8,128)(2,1)}), bf16[8,256,576]{1,2,0:T(8,128)(2,1)}, u32[]{:S(2)}, u32[]{:S(2)}) async-start(bf16[8,256,576]{1,2,0:T(8,128)(2,1)} %bitcast.10), calls=%async_computation | async-start | bytes 4718592 | tf_op jit(solution)/shard_map/all_to_all | solution.py:481
  224.3 43.1 %all_gather.23 = bf16[1024,64]{0,1:T(8,128)(2,1)S(1)} all-gather(bf16[256,64]{0,1:T(8,128)(2,1)S(1)} %fusion.13), channel_id=1, replica_groups=mesh['grp'=4,'fsdp'=4,'tp'=2] {'fsdp'}, dimensions={0}, use_global_device_ids=true | all-gather | bytes 163840 | tf_op jit(solution)/shard_map/all_gather | solution.py:420
  267.5 2.7 copy.47
  270.1 2.3 fusion.40
  272.6 2.1 reduce.1
  275.8 25.1 %line_sum.3.x_ref = f32[768,128]{1,0:T(8,128)S(1)} custom-call(f32[768,128]{1,0:T(8,128)S(1)} %pad_maximum_fusion.1.x_ref), custom_call_target="tpu_custom_call" | custom-call | tf_op jit(solution)/shard_map/line_sum/pallas_call | solution.py:240
  301.7 17.4 %fsdp_gather.1 = f32[4,768,128]{2,1,0:T(8,128)} custom-call(f32[768,128]{1,0:T(8,128)} %copy-done.5), custom_call_target="tpu_custom_call" | custom-call | tf_op jit(solution)/shard_map/fsdp_gather/pallas_call | solution.py:304
  319.1 1.4 copy-done.8
  321.2 1.7 reshape.113
  322.9 3.1 copy.50
  326.0 19.6 %product.1 = f32[1280,4096]{1,0:T(8,128)} custom-call(bf16[1280,768]{1,0:T(8,128)(2,1)S(1)} %bitcast.62, bf16[768,4096]{1,0:T(8,128)(2,1)} %all-gather.6.cloned.1.call-done.b_ref), custom_call_target="tpu_custom_call" | custom-call | tf_op jit(solution)/shard_map/product/pallas_call | solution.py:323
  (69 shorter events, 11.5 us)
Async XLA Ops:
  7.2 92.0 %copy-start = (bf16[2048,64]{0,1:T(8,128)(2,1)S(1)}, bf16[2048,64]{0,1:T(8,128)(2,1)}, u32[]{:S(2)}) copy-start(bf16[2048,64]{0,1:T(8,128)(2,1)} %param.17) | copy-start | bytes 786436
  7.2 18.7 %copy-start.6 = (bf16[192,1280]{1,0:T(8,128)(2,1)S(1)}, bf16[192,1280]{1,0:T(8,128)(2,1)}, u32[]{:S(2)}) copy-start(bf16[192,1280]{1,0:T(8,128)(2,1)} %frames_ref.1) | copy-start | bytes 1474564
  7.2 91.9 %all-reduce.3.cloned.1.call-start = ((), (), s32[]{:S(2)}) async-start(), calls=%async_computation.1 | async-start | bytes 786432 | tf_op jit(solution)/shard_map/psum | solution.py:421
  20.9 0.7 copy-start.9
  25.8 146.5 %all-gather.4.cloned.1.call-start = ((), (), s32[]{:S(2)}) async-start(), calls=%async_computation.2 | async-start | bytes 1966080 | tf_op jit(solution)/shard_map/all_gather | solution.py:426
  97.7 1.3 copy-start.2
  99.1 1.5 copy-start.4
  99.1 226.9 %all-gather.6.cloned.1.call-start = ((), (), s32[]{:S(2)}) async-start(), calls=%async_computation.3 | async-start | bytes 7864320 | tf_op jit(solution)/shard_map/all_gather | solution.py:463
  99.2 78.7 %collective-permute-start = (bf16[1024,64]{0,1:T(8,128)(2,1)S(1)}, bf16[1024,64]{0,1:T(8,128)(2,1)S(1)}, u32[]{:S(2)}, u32[]{:S(2)}) collective-permute-start(bf16[1024,64]{0,1:T(8,128)(2,1)S(1)} %constant_dynamic-slice_fusion), channel_id=1, source_target_pairs={{0,0},{1,2},{2,4},{3,6},{4,1},{5,3},{6,5},{7,7},{8,8},{9,10},{10,1... | collective-permute-start | bytes 393224 | tf_op jit(solution)/shard_map/ppermute | solution.py:385
  104.5 64.7 %copy-start.3 = (bf16[1024,1024]{1,0:T(8,128)(2,1)S(1)}, bf16[1024,1024]{1,0:T(8,128)(2,1)}, u32[]{:S(2)}) copy-start(bf16[1024,1024]{1,0:T(8,128)(2,1)} %copy-done.2) | copy-start | bytes 6291460
  205.0 4.9 %copy-start.7 = (bf16[1024,1024]{1,0:T(8,128)(2,1)}, bf16[1024,1024]{1,0:T(8,128)(2,1)S(1)}, u32[]{:S(2)}) copy-start(bf16[1024,1024]{1,0:T(8,128)(2,1)S(1)} %fusion.1) | copy-start | bytes 6291460
  205.0 2.5 copy-start.11
  219.6 53.0 %all-to-all-start = ((bf16[8,256,576]{1,2,0:T(8,128)(2,1)}), bf16[8,256,576]{1,2,0:T(8,128)(2,1)}, u32[]{:S(2)}, u32[]{:S(2)}) async-start(bf16[8,256,576]{1,2,0:T(8,128)(2,1)} %bitcast.10), calls=%async_computation | async-start | bytes 4718592 | tf_op jit(solution)/shard_map/all_to_all | solution.py:481
  272.5 3.1 copy-start.10
  300.9 0.7 copy-start.5
  319.1 1.4 copy-start.8
  319.1 2.1 slice-start
  326.0 19.6 %copy-start.1 = (bf16[2048,64]{0,1:T(8,128)(2,1)S(1)}, bf16[2048,64]{0,1:T(8,128)(2,1)}, u32[]{:S(2)}) copy-start(bf16[2048,64]{0,1:T(8,128)(2,1)} %param.17) | copy-start | bytes 786436
Sparse Core Ops, SparseCore 0:
  25.9 37.2 all-reduce.2
  99.2 32.9 all-gather.3
  201.8 86.7 all-gather.5

commit v3 on v2

--- a/solution.py
+++ b/solution.py
@@ -29,55 +29,37 @@
     )
 
 
-def greet_plane(f_size, t_size):
+def greet_plane(f_size, t_size, barrier):
     me = lax.axis_index("fsdp") * t_size + lax.axis_index("tp")
-    barrier = pltpu.get_barrier_semaphore()
     for k in range(1, f_size * t_size):
         p = lax.rem(me + k, f_size * t_size)
         where = {"fsdp": lax.div(p, t_size), "tp": lax.rem(p, t_size)}
         pl.semaphore_signal(barrier, inc=1, device_id=where, device_id_type=MESH)
-    pl.semaphore_wait(barrier, f_size * t_size - 1)
-
-
-def exchange_kernel(
-    f_size,
-    t_size,
-    frames_ref,
-    text_ref,
-    frozen_ref,
-    frames_out,
-    text_out,
-    frozen_out,
-    send_a,
-    recv_a,
-    send_b,
-    recv_b,
-    send_w,
-    recv_w,
-    local,
-):
+
+
+def start_exchange(f_size, t_size, text_ref, frozen_ref, text_out, frozen_out, sems):
+    send_b, recv_b, send_w, recv_w, local = sems
     f, t = lax.axis_index("fsdp"), lax.axis_index("tp")
-    rows = frames_ref.shape[0]
     tok = text_ref.shape[0]
     cols = text_out.shape[1]
     v = frozen_ref.shape[1]
-    greet_plane(f_size, t_size)
 
     def columns(i, size):
         return pl.ds(pl.multiple_of(i * size, 128), size)
 
+    weights = []
+    for j in range(t_size):
+        b = f * t_size + j
+        d_f, d_t = lax.rem(b, f_size), lax.div(b, f_size)
+        mine = jnp.logical_and(d_f == f, d_t == t)
+        src = frozen_ref.at[pl.ds(j * cols, cols)]
+        dst = frozen_out.at[:, columns(t, v)]
+        far = push(src, dst, send_w.at[j], recv_w.at[t], {"fsdp": d_f, "tp": d_t})
+        near = pltpu.make_async_copy(src, dst, local.at[1])
+        weights.append((mine, far, near))
+        pl.when(jnp.logical_not(mine))(far.start)
+        pl.when(mine)(near.start)
     copies = []
-    for k in range(1, f_size):
-        p = lax.rem(f + k, f_size)
-        copies.append(
-            push(
-                frames_ref,
-                frames_out.at[pl.ds(f * rows, rows)],
-                send_a.at[k - 1],
-                recv_a.at[k - 1],
-                {"fsdp": p},
-            )
-        )
     for k in range(1, f_size):
         p = lax.rem(f + k, f_size)
         copies.append(
@@ -89,69 +71,74 @@
                 {"fsdp": p},
             )
         )
-    for c in copies:
-        c.start()
-    own = [
-        pltpu.make_async_copy(frames_ref, frames_out.at[pl.ds(f * rows, rows)], local.at[0]),
-        pltpu.make_async_copy(
-            text_ref.at[:, columns(f, cols)], text_out.at[pl.ds(f * tok, tok)], local.at[1]
-        ),
-    ]
-    for c in own:
-        c.start()
-    weights = []
-    for j in range(t_size):
-        b = f * t_size + j
-        d_f, d_t = lax.rem(b, f_size), lax.div(b, f_size)
-        mine = jnp.logical_and(d_f == f, d_t == t)
-        src = frozen_ref.at[pl.ds(j * cols, cols)]
-        dst = frozen_out.at[:, columns(t, v)]
-        far = push(src, dst, send_w.at[j], recv_w.at[t], {"fsdp": d_f, "tp": d_t})
-        near = pltpu.make_async_copy(src, dst, local.at[2])
-        weights.append((mine, far, near))
-        pl.when(jnp.logical_not(mine))(far.start)
-        pl.when(mine)(near.start)
-    for c in own:
-        c.wait()
-    for c in copies:
-        c.wait_recv()
-        c.wait_send()
-    for mine, far, near in weights:
-        pl.when(jnp.logical_not(mine))(far.wait_send)
-        pl.when(mine)(near.wait)
-    source = lax.div(t * f_size + f, t_size)
-    for ts in range(t_size):
-        arrive = push(
-            frozen_ref.at[pl.ds(0, cols)],
-            frozen_out.at[:, pl.ds(ts * v, v)],
-            send_w.at[0],
-            recv_w.at[ts],
-            {"fsdp": lax.rem(f + 1, f_size)},
+        copies[-1].start()
+    own = pltpu.make_async_copy(
+        text_ref.at[:, columns(f, cols)], text_out.at[pl.ds(f * tok, tok)], local.at[0]
+    )
+    own.start()
+
+    def finish():
+        own.wait()
+        for c in copies:
+            c.wait_recv()
+            c.wait_send()
+        for mine, far, near in weights:
+            pl.when(jnp.logical_not(mine))(far.wait_send)
+            pl.when(mine)(near.wait)
+        source = lax.div(t * f_size + f, t_size)
+        for ts in range(t_size):
+            arrive = push(
+                frozen_ref.at[pl.ds(0, cols)],
+                frozen_out.at[:, pl.ds(ts * v, v)],
+                send_w.at[0],
+                recv_w.at[ts],
+                {"fsdp": lax.rem(f + 1, f_size)},
+            )
+            pl.when(jnp.logical_not(jnp.logical_and(source == f, t == ts)))(arrive.wait_recv)
+
+    return finish
+
+
+def sum_and_exchange_kernel(
+    n, chunks, f_size, t_size, x_ref, text_ref, frozen_ref, o_ref, text_out, frozen_out, *scratch
+):
+    def start():
+        return start_exchange(
+            f_size, t_size, text_ref, frozen_ref, text_out, frozen_out, scratch[8:]
         )
-        pl.when(jnp.logical_not(jnp.logical_and(source == f, t == ts)))(arrive.wait_recv)
-
-
-def exchange(frames, text, frozen, f_size, t_size):
+
+    line_kernel(n, chunks, x_ref, o_ref, *scratch[:8], plane_sizes=(f_size, t_size), extra=start)
+
+
+def sum_and_exchange(x, text, frozen, n, f_size, t_size, chunks):
     cols = text.shape[1] // f_size
     return pl.pallas_call(
-        functools.partial(exchange_kernel, f_size, t_size),
+        functools.partial(sum_and_exchange_kernel, n, chunks, f_size, t_size),
         out_shape=(
-            jax.ShapeDtypeStruct((frames.shape[0] * f_size, frames.shape[1]), frames.dtype),
+            jax.ShapeDtypeStruct(x.shape, x.dtype),
             jax.ShapeDtypeStruct((text.shape[0] * f_size, cols), text.dtype),
             jax.ShapeDtypeStruct((cols, frozen.shape[1] * t_size), frozen.dtype),
         ),
         in_specs=[VMEM] * 3,
         out_specs=(VMEM,) * 3,
-        scratch_shapes=[DMA((f_size - 1,))] * 4 + [DMA((t_size,))] * 2 + [DMA((3,))],
+        scratch_shapes=[pltpu.VMEM(x.shape, x.dtype)] * 4
+        + [DMA((chunks,))] * 4
+        + [DMA((f_size - 1,))] * 2
+        + [DMA((t_size,))] * 2
+        + [DMA((2,))],
         compiler_params=pltpu.CompilerParams(
-            collective_id=0, has_side_effects=True, vmem_limit_bytes=VMEM_LIMIT
+            collective_id=1, has_side_effects=True, vmem_limit_bytes=VMEM_LIMIT
         ),
-        name="exchange",
-    )(frames, text, frozen)
-
-
-def line_kernel(n, chunks, x_ref, o_ref, from_left, from_right, to_right, to_left, *sems):
+        name="sum_and_exchange",
+    )(x, text, frozen)
+
+
+LAG = 2
+
+
+def line_kernel(n, chunks, x_ref, o_ref, from_left, from_right, to_right, to_left, *sems, **more):
     send_r, recv_r, send_l, recv_l = sems
+    plane_sizes, extra = more.get("plane_sizes"), more.get("extra")
     g = lax.axis_index("grp")
     rows = x_ref.shape[0] // chunks
     right, left = jnp.minimum(g + 1, n - 1), jnp.maximum(g - 1, 0)
@@ -166,7 +153,12 @@
     def _():
         pl.semaphore_signal(barrier, inc=1, device_id={"grp": right}, device_id_type=MESH)
 
-    pl.semaphore_wait(barrier, has_left.astype(jnp.int32) + has_right.astype(jnp.int32))
+    expected = has_left.astype(jnp.int32) + has_right.astype(jnp.int32)
+    if extra is not None:
+        greet_plane(*plane_sizes, barrier)
+        expected = expected + plane_sizes[0] * plane_sizes[1] - 1
+    pl.semaphore_wait(barrier, expected)
+    end_extra = extra() if extra is not None else None
 
     def part(c):
         return pl.ds(pl.multiple_of(c * rows, rows), rows)
@@ -200,11 +192,11 @@
             copy(c).start()
 
     def body(i, carry):
-        step(i - g, has_left, has_right, rightward, from_left, to_right)
-        step(i - (n - 1 - g), has_right, has_left, leftward, from_right, to_left)
+        step(i - LAG * g, has_left, has_right, rightward, from_left, to_right)
+        step(i - LAG * (n - 1 - g), has_right, has_left, leftward, from_right, to_left)
         return carry
 
-    lax.fori_loop(0, chunks + n - 1, body, 0)
+    lax.fori_loop(0, chunks + LAG * (n - 1), body, 0)
 
     def finish(c, carry):
         @pl.when(jnp.logical_not(has_left))
@@ -234,6 +226,8 @@
         return carry
 
     lax.fori_loop(0, chunks, finish, 0)
+    if end_extra is not None:
+        end_extra()
 
 
 def line_sum(x, n, chunks, collective_id):
@@ -253,7 +247,9 @@
 def plane_sum_kernel(f_size, t_size, x_ref, o_ref, slots, send, recv):
     count = f_size * t_size
     me = lax.axis_index("fsdp") * t_size + lax.axis_index("tp")
-    greet_plane(f_size, t_size)
+    barrier = pltpu.get_barrier_semaphore()
+    greet_plane(f_size, t_size, barrier)
+    pl.semaphore_wait(barrier, count - 1)
     copies = []
     for k in range(1, count):
         p = lax.rem(me + k, count)
@@ -282,7 +278,8 @@
     )(x)
 
 
-def gather_kernel(f_size, x_ref, o_ref, send, recv):
+def gather_kernel(f_size, count, *refs):
+    ins, outs, sems = refs[:count], refs[count : 2 * count], refs[2 * count :]
     f = lax.axis_index("fsdp")
     barrier = pltpu.get_barrier_semaphore()
     for k in range(1, f_size):
@@ -290,26 +287,32 @@
         pl.semaphore_signal(barrier, inc=1, device_id=where, device_id_type=MESH)
     pl.semaphore_wait(barrier, f_size - 1)
     copies = []
-    for k in range(1, f_size):
-        where = {"fsdp": lax.rem(f + k, f_size)}
-        copies.append(push(x_ref, o_ref.at[f], send.at[k - 1], recv.at[k - 1], where))
-        copies[-1].start()
-    o_ref[f] = x_ref[...]
+    for i in range(count):
+        send, recv = sems[2 * i], sems[2 * i + 1]
+        for k in range(1, f_size):
+            where = {"fsdp": lax.rem(f + k, f_size)}
+            copies.append(push(ins[i], outs[i].at[f], send.at[k - 1], recv.at[k - 1], where))
+            copies[-1].start()
+    for i in range(count):
+        outs[i][f] = ins[i][...]
     for c in copies:
         c.wait_recv()
         c.wait_send()
 
 
-def fsdp_gather(x, f_size, collective_id):
+def fsdp_gather(arrays, f_size, collective_id):
+    count = len(arrays)
     return pl.pallas_call(
-        functools.partial(gather_kernel, f_size),
-        out_shape=jax.ShapeDtypeStruct((f_size,) + x.shape, x.dtype),
-        in_specs=[VMEM],
-        out_specs=VMEM,
-        scratch_shapes=[DMA((f_size - 1,)), DMA((f_size - 1,))],
-        compiler_params=pltpu.CompilerParams(collective_id=collective_id, has_side_effects=True),
+        functools.partial(gather_kernel, f_size, count),
+        out_shape=tuple(jax.ShapeDtypeStruct((f_size,) + x.shape, x.dtype) for x in arrays),
+        in_specs=[VMEM] * count,
+        out_specs=(VMEM,) * count,
+        scratch_shapes=[DMA((f_size - 1,))] * (2 * count),
+        compiler_params=pltpu.CompilerParams(
+            collective_id=collective_id, has_side_effects=True, vmem_limit_bytes=VMEM_LIMIT
+        ),
         name="fsdp_gather",
-    )(x)
+    )(*arrays)
 
 
 def product_kernel(a_ref, b_ref, o_ref):
@@ -417,23 +420,27 @@
     )
     grad_full, up_full = both[:tok], both[tok:]
     lora_tok = (adapter_scale * contract_trailing(grad_full, up_full)).astype(jnp.bfloat16)
-    lora_plane = lax.all_gather(lora_tok, "fsdp", axis=0, tiled=True)
     grad_rows = lax.psum(contract_leading(take_own, grad_full).astype(jnp.bfloat16), "grp")
 
-    frames_all, text, frozen_own = exchange(frames, text_token_embedding, frozen, f_size, t_size)
-    text = text.reshape(f_size, tok, cols)
+    frames_all, lora_plane = fsdp_gather((frames, lora_tok), f_size, 0)
+    frames_all = frames_all.reshape(f_size * block_frames, frames.shape[1])
+    lora_plane = lora_plane.reshape(f_size * tok, rank)
     grad_rows, frames_all = lax.optimization_barrier((grad_rows, frames_all))
     grad_rows = lax.all_gather(grad_rows, "fsdp", axis=0, tiled=True)
+
+    projector_own = lax.dynamic_slice_in_dim(projector, f_idx * cols, cols, 1)
+    embedded, text, frozen_own = sum_and_exchange(
+        jnp.dot(frames_all, projector_own, preferred_element_type=jnp.float32).astype(jnp.bfloat16),
+        text_token_embedding,
+        frozen,
+        lax.axis_size("grp"),
+        f_size,
+        t_size,
+        16,
+    )
+    text = text.reshape(f_size, tok, cols)
     lora_rows = (adapter_scale * contract_trailing(grad_rows, up_full)).astype(jnp.bfloat16)
     grad_norm = contract_trailing(grad_rows, frozen_own) + contract_trailing(lora_rows, down_own)
-
-    projector_own = lax.dynamic_slice_in_dim(projector, f_idx * cols, cols, 1)
-    embedded = line_sum(
-        jnp.dot(frames_all, projector_own, preferred_element_type=jnp.float32).astype(jnp.bfloat16),
-        lax.axis_size("grp"),
-        16,
-        1,
-    )
     audio = lax.dot_general(
         take,
         embedded.reshape(f_size, block_frames, cols),
@@ -469,16 +476,15 @@
     value_part = value_part + adapter_scale * jnp.dot(
         low_part.astype(jnp.bfloat16), up_full, preferred_element_type=jnp.float32
     )
-    value_part = value_part.astype(jnp.bfloat16).reshape(f_size, tok, t_size, v_shard)
+    value_part = value_part.astype(jnp.bfloat16).reshape(f_size * tok, t_size, v_shard)
     low_send = jnp.broadcast_to(
-        low_part.astype(jnp.bfloat16).reshape(f_size, tok, 1, rank), (f_size, tok, t_size, rank)
-    )
-    sent = (
-        jnp.concatenate([value_part, low_send], axis=3)
-        .transpose(0, 2, 1, 3)
-        .reshape(f_size * t_size, tok, v_shard + rank)
-    )
-    got = lax.all_to_all(sent, plane, split_axis=0, concat_axis=0, tiled=True)
+        low_part.astype(jnp.bfloat16)[:, None, :], (f_size * tok, t_size, rank)
+    )
+    sent = jnp.concatenate([value_part, low_send], axis=2).transpose(1, 0, 2)
+    got = lax.all_to_all(sent, "tp", split_axis=0, concat_axis=0, tiled=True)
+    pair = jnp.sum(got.astype(jnp.float32), axis=0).astype(jnp.bfloat16)
+    pair = pair.reshape(f_size, tok, v_shard + rank)
+    got = lax.all_to_all(pair, "fsdp", split_axis=0, concat_axis=0, tiled=True)
     total = jnp.sum(got.astype(jnp.float32), axis=0)
     value_output = total[:, :v_shard].astype(jnp.bfloat16)
     low_half = total[:, v_shard:].astype(jnp.bfloat16)
@@ -487,7 +493,8 @@
     down_part = contract_leading(normed, lora_plane)
     both_parts = jnp.concatenate([down_part.reshape(-1, 128), up_part.reshape(-1, 128)], axis=0)
     summed = line_sum(both_parts, lax.axis_size("grp"), 4, 3)
-    gathered = fsdp_gather(summed, f_size, 4)
+    (gathered,) = fsdp_gather((summed.astype(jnp.bfloat16),), f_size, 4)
+    gathered = gathered.astype(jnp.float32)
     split = cols * rank // 128
     down_map_gradient = gathered[:, :split].reshape(width, rank)
     up_map_gradient = jnp.sum(gathered[:, split:], axis=0).reshape(rank, v_shard)

time: 353 us -> 275 us (0.78)
  Pallas kernels: 211 us -> 153 us
  blocking collectives: 55.1 us -> 17.6 us
  waiting for transfers between devices: 0.06 us -> 22.8 us
  local copies, waits for them, and re-layouts: 23.3 us -> 14.3 us
    pallas_call x2 -> x1, Pallas kernels: 89.8 us -> 20 us  [line_sum(): pl.pallas_call(functools.partial(line_kernel, n, chunks), out_shape=jax.S...]
    all_gather x1 -> x0, blocking collectives: 43.1 us -> none  [shards(): lora_plane = lax.all_gather(lora_tok, 'fsdp', axis=0, tiled=True)]
    pallas_call x2 -> x3, Pallas kernels: 89.2 us -> 107 us  [the longest x1 59.5 us: sum_and_exchange(): pl.pallas_call(functools.partial(sum_and_exchange_kernel, n, chunks, f_si...]
    all_to_all x1, waiting for transfers between devices: 0.01 us -> 11 us  [shards(): got = lax.all_to_all(pair, 'fsdp', split_axis=0, concat_axis=0, tiled=True)]
    psum x1, waiting for transfers between devices: 0.01 us -> 9.23 us  [shards(): lax.psum(contract_leading(take_own, grad_full).astype(jnp.bfloat16), 'grp')]
    pallas_call x1, Pallas kernels: 12.4 us -> 6.31 us  [plane_sum(): pl.pallas_call(functools.partial(plane_sum_kernel, f_size, t_size), out_s...]
    all_to_all x0 -> x1, blocking collectives: none -> 5.63 us  [shards(): got = lax.all_to_all(sent, 'tp', split_axis=0, concat_axis=0, tiled=True)]
    reshape x2 -> x1, local copies, waits for them, and re-layouts: 7.43 us -> 2.37 us  [shards(): pair = pair.reshape(f_size, tok, v_shard + rank)]
  transfers between devices with their start and end apart: 5 -> 5, of which waited for: 0 -> 3; matrix products, arithmetic and copies ran while one was open for 12% -> 16% of each run, Pallas kernels for 51% -> 47%
where the time goes in v3:
time: 275 us; the launch traced here: 274 us
  Pallas kernels  153 us (56%)
  matrix products  27.2 us (10%)
  waiting for transfers between devices  22.8 us (8%)
  other arithmetic  19.4 us (7%)
  blocking collectives  17.6 us (6%)
  local copies, waits for them, and re-layouts  14.3 us (5%)
  between operations  14.1 us (5%)
  starting transfers between devices  5.27 us (2%)
    pallas_call x1, Pallas kernels, sum_and_exchange(): pl.pallas_call(functools.partial(sum_and_exchange_kernel, n, chunks, f_si...  59.5 us
    pallas_call x2, Pallas kernels, fsdp_gather(): pl.pallas_call(functools.partial(gather_kernel, f_size, count), out_shape...  47.7 us
    pallas_call x1, Pallas kernels, line_sum(): pl.pallas_call(functools.partial(line_kernel, n, chunks), out_shape=jax.S...  20 us
    pallas_call x1, Pallas kernels, product(): pl.pallas_call(product_kernel, out_shape=jax.ShapeDtypeStruct((m, n), jnp...  19.6 us
    dot_general x3, matrix products, contract_trailing(): lax.dot_general(left_side, right_side, (((1,), (1,)), ((), ())), preferre...  11.5 us
    all_to_all x1, waiting for transfers between devices, shards(): got = lax.all_to_all(pair, 'fsdp', split_axis=0, concat_axis=0, tiled=True)  11 us
    all_gather x1, blocking collectives, shards(): lax.all_gather(jnp.stack([clip_frame_length[0], audio_first_token[0]]), '...  9.66 us
    psum x1, waiting for transfers between devices, shards(): lax.psum(contract_leading(take_own, grad_full).astype(jnp.bfloat16), 'grp')  9.23 us
  transfers between devices with their start and end apart: 5, of which 3 were waited for; matrix products, arithmetic and copies ran while one was open for 16% of the time, Pallas kernels for 47%

profile of v3, /device:TPU:0, one launch (start us, length us, event | category | flops | bytes accessed | tf_op | source)
XLA Modules:
  0.0 273.7 jit_solution(2946378347984408403)
XLA Ops:
  8.8 9.7 %all-gather = s32[8,4,4]{2,1,0:T(4,128)S(1)} all-gather(s32[2,4,4]{2,1,0:T(4,128)S(1)} %pad_add_fusion), channel_id=2, replica_groups=mesh['grp'=4,'fsdp'=4,'tp'=2] {'fsdp'}, dimensions={0}, use_global_device_ids=true | all-gather | bytes 640 | tf_op jit(solution)/shard_map/all_gather | solution.py:387
  19.8 1.1 broadcast_multiply_fusion
  21.8 2.3 all_gather.17
  25.5 27.7 %fsdp_gather.2 = (bf16[4,192,1280]{2,1,0:T(8,128)(2,1)S(1)}, bf16[4,256,64]{2,1,0:T(8,128)(2,1)S(1)}) custom-call(bf16[192,1280]{1,0:T(8,128)(2,1)S(1)} %copy-done.3, bf16[256,64]{1,0:T(8,128)(2,1)S(1)} %fusion.18.refs_1_), custom_call_target="tpu_custom_call" | custom-call | tf_op jit(solution)/shard_map/fsdp_gather/pallas_call | solution.py:305
  53.2 9.2 %all-reduce.3.cloned.1.call-done = bf16[192,1024]{1,0:T(8,128)(2,1)} async-done(((bf16[192,1024]{1,0:T(8,128)(2,1)}), bf16[192,1024]{1,0:T(8,128)(2,1)}) %all-reduce.3.cloned.1.call-update) | async-done | bytes 393232 | tf_op jit(solution)/shard_map/psum | solution.py:423
  63.9 3.9 %fusion.13.x_ref = bf16[768,1024]{1,0:T(8,128)(2,1)S(1)} fusion(bf16[768,1280]{1,0:T(8,128)(2,1)S(1)} %bitcast.65, bf16[1280,4096]{1,0:T(8,128)(2,1)} %param.13, s32[]{:T(128)S(6)} %select_n.50), kind=kOutput, calls=%fused_computation.23 | convolution fusion | flops 2014052352 | bytes 6160388 | tf_op jit(solution)/shard_map/dot_general | solution.py:433
  67.8 59.5 %sum_and_exchange.1 = (bf16[768,1024]{1,0:T(8,128)(2,1)S(1)}, bf16[1024,1024]{1,0:T(8,128)(2,1)S(1)}, bf16[1024,1024]{1,0:T(8,128)(2,1)}) custom-call(bf16[768,1024]{1,0:T(8,128)(2,1)S(1)} %fusion.13.x_ref, bf16[256,4096]{1,0:T(8,128)(2,1)} %text_ref.1, bf16[2048,512]{1,0:T(8,128)(2,1)} %frozen_ref.1), custom_call_target="tpu_custom_call" | custom-call | tf_op jit(solution)/shard_map/sum_and_exchange/pallas_call | solution.py:115
  127.4 2.4 multiply_reduce_fusion
  129.8 2.5 all-gather.4.cloned.1.call-done
  132.3 5.6 %fusion.44 = f32[768,1024]{1,0:T(8,128)} fusion(bf16[768,1024]{1,0:T(8,128)(2,1)} %all-gather.4.cloned.1.call-done, bf16[1024,1024]{1,0:T(8,128)(2,1)} %get-tuple-element.16), kind=kOutput, calls=%fused_computation.80 | convolution fusion | flops 1610612736 | bytes 6815744 | tf_op jit(solution)/shard_map/dot_general | solution.py:347
  137.9 5.7 %fusion.2 = (f32[768]{0:T(1024)S(1)}, f32[768]{0:T(1024)S(1)}, f32[768,1024]{1,0:T(8,128)}) fusion(bf16[768,1024]{1,0:T(8,128)(2,1)S(1)} %get-tuple-element.13, f32[1024]{0:T(1024)S(1)} %dynamic_slice.15, f32[768,1024]{1,0:T(8,128)} %fusion.44, bf16[1024,64]{0,1:T(8,128)(2,1)S(1)} %collective-permute-done, ...), kind=kOutput, calls=%fused_computation.9 | convolution fusion | flops 206928384 | bytes 9709568 | tf_op jit(solution)/shard_map/dot_general | solution.py:347
  144.1 6.3 %plane_sum.1 = f32[24,128]{1,0:T(8,128)} custom-call(f32[24,128]{1,0:T(8,128)} %fusion.32.x_ref), custom_call_target="tpu_custom_call" | custom-call | tf_op jit(solution)/shard_map/plane_sum/pallas_call | solution.py:270
  151.9 3.7 %fusion.6 = bf16[768,1024]{1,0:T(8,128)(2,1)} fusion(bf16[768,1024]{1,0:T(8,128)(2,1)S(1)} %get-tuple-element.13, f32[768,1024]{1,0:T(8,128)} %get-tuple-element.51, f32[768]{0:T(1024)S(1)} %fusion.35, f32[768]{0:T(1024)S(1)} %rsqrt_bitcast_fusion, f32[1024]{0:T(1024)S(1)} %dynamic_slice.15), kind=kLoop, calls=%fused_computation.13 | loop fusion | flops 4718592 | bytes 6301696 | tf_op jit(solution)/shard_map/convert_element_type | solution.py:469
  156.3 2.1 fusion.1
  160.1 2.4 fusion.45
  162.4 1.7 add_convert_fusion
  164.4 5.6 %all_to_all.10 = bf16[2,1024,576]{1,2,0:T(8,128)(2,1)S(1)} all-to-all(bf16[2,1024,576]{1,2,0:T(8,128)(2,1)S(1)} %maximum_bitcast_fusion), channel_id=1, replica_groups=mesh['grp'=4,'fsdp'=4,'tp'=2] {'tp'}, dimensions={0} | all-to-all | bytes 4718592 | tf_op jit(solution)/shard_map/all_to_all | solution.py:484
  170.0 1.8 reduce_sum.113
  171.8 2.4 copy.87
  174.2 4.5 %all-to-all-start.1 = ((bf16[4,256,576]{1,2,0:T(8,128)(2,1)}), bf16[4,256,576]{1,2,0:T(8,128)(2,1)}, u32[]{:S(2)}, u32[]{:S(2)}) async-start(bf16[4,256,576]{1,2,0:T(8,128)(2,1)} %bitcast.61), calls=%async_computation.1 | async-start | bytes 2359296 | tf_op jit(solution)/shard_map/all_to_all | solution.py:487
  178.7 2.7 copy.69
  181.4 3.4 %fusion.16 = f32[1024,64]{1,0:T(8,128)} fusion(bf16[4,256,64]{2,1,0:T(8,128)(2,1)S(1)} %get-tuple-element.17, bf16[4,256,1024]{2,1,0:T(8,128)(2,1)} %get-tuple-element.53, f32[1024]{0:T(1024)S(1)} %dynamic_slice.15, f32[4,256]{1,0:T(4,128)S(1)} %rsqrt.31), kind=kOutput, calls=%fused_computation.25 | convolution fusion | flops 138412032 | bytes 2498560 | tf_op jit(solution)/shard_map/dot_general | solution.py:341
  184.8 1.2 reshape.131
  185.9 11.0 %all-to-all-done.1 = bf16[4,256,576]{1,2,0:T(8,128)(2,1)} async-done(((bf16[4,256,576]{1,2,0:T(8,128)(2,1)}), bf16[4,256,576]{1,2,0:T(8,128)(2,1)}, u32[]{:S(2)}, u32[]{:S(2)}) %all-to-all-start.1) | async-done | bytes 1179680 | tf_op jit(solution)/shard_map/all_to_all | solution.py:487
  197.0 1.6 reduce.2
  198.8 20.0 %line_sum.1 = f32[768,128]{1,0:T(8,128)S(1)} custom-call(f32[768,128]{1,0:T(8,128)S(1)} %pad_maximum_fusion.x_ref), custom_call_target="tpu_custom_call" | custom-call | tf_op jit(solution)/shard_map/line_sum/pallas_call | solution.py:234
  218.8 20.0 %fsdp_gather.3 = bf16[4,768,128]{2,1,0:T(8,128)(2,1)S(1)} custom-call(bf16[768,128]{1,0:T(8,128)(2,1)S(1)} %convert_element_type.83.refs_0_), custom_call_target="tpu_custom_call" | custom-call | tf_op jit(solution)/shard_map/fsdp_gather/pallas_call | solution.py:305
  239.0 1.2 convert_element_type.84
  241.1 1.1 slice_reduce_fusion
  242.8 1.7 reshape.133
  244.5 3.1 %copy.73 = f32[4096,64]{0,1:T(8,128)} copy(f32[4096,64]{1,0:T(8,128)} %reshape.133) | data formatting | bytes 2097152
  247.6 19.6 %product.1 = f32[1280,4096]{1,0:T(8,128)} custom-call(bf16[1280,768]{1,0:T(8,128)(2,1)S(1)} %bitcast.63, bf16[768,4096]{1,0:T(8,128)(2,1)} %all-gather.6.cloned.1.call-done.b_ref), custom_call_target="tpu_custom_call" | custom-call | tf_op jit(solution)/shard_map/product/pallas_call | solution.py:326
  (61 shorter events, 13.0 us)
Async XLA Ops:
  7.2 55.3 %copy-start = (bf16[2048,64]{0,1:T(8,128)(2,1)S(1)}, bf16[2048,64]{0,1:T(8,128)(2,1)}, u32[]{:S(2)}) copy-start(bf16[2048,64]{0,1:T(8,128)(2,1)} %param.17) | copy-start | bytes 786436
  7.2 55.2 %all-reduce.3.cloned.1.call-start = ((), (), s32[]{:S(2)}) async-start(), calls=%async_computation.2 | async-start | bytes 786432 | tf_op jit(solution)/shard_map/psum | solution.py:423
  20.9 4.6 %copy-start.3 = (bf16[192,1280]{1,0:T(8,128)(2,1)S(1)}, bf16[192,1280]{1,0:T(8,128)(2,1)}, u32[]{:S(2)}) copy-start(bf16[192,1280]{1,0:T(8,128)(2,1)} %refs_0_.1) | copy-start | bytes 1474564
  24.1 1.1 copy-start.4
  25.1 107.2 %all-gather.4.cloned.1.call-start = ((), (), s32[]{:S(2)}) async-start(), calls=%async_computation.3 | async-start | bytes 1966080 | tf_op jit(solution)/shard_map/all_gather | solution.py:429
  53.2 10.7 %copy-start.2 = (bf16[4,192,1280]{2,1,0:T(8,128)(2,1)}, bf16[4,192,1280]{2,1,0:T(8,128)(2,1)S(1)}, u32[]{:S(2)}) copy-start(bf16[4,192,1280]{2,1,0:T(8,128)(2,1)S(1)} %get-tuple-element.11) | copy-start | bytes 5898244
  62.4 185.2 %all-gather.6.cloned.1.call-start = ((), (), s32[]{:S(2)}) async-start(), calls=%async_computation.4 | async-start | bytes 7864320 | tf_op jit(solution)/shard_map/all_gather | solution.py:470
  62.5 75.4 %collective-permute-start = (bf16[1024,64]{0,1:T(8,128)(2,1)S(1)}, bf16[1024,64]{0,1:T(8,128)(2,1)S(1)}, u32[]{:S(2)}, u32[]{:S(2)}) collective-permute-start(bf16[1024,64]{0,1:T(8,128)(2,1)S(1)} %constant_dynamic-slice_fusion), channel_id=1, source_target_pairs={{0,0},{1,2},{2,4},{3,6},{4,1},{5,3},{6,5},{7,7},{8,8},{9,10},{10,1... | collective-permute-start | bytes 393224 | tf_op jit(solution)/shard_map/ppermute | solution.py:388
  158.5 1.6 copy-start.6
  174.2 22.7 %all-to-all-start.1 = ((bf16[4,256,576]{1,2,0:T(8,128)(2,1)}), bf16[4,256,576]{1,2,0:T(8,128)(2,1)}, u32[]{:S(2)}, u32[]{:S(2)}) async-start(bf16[4,256,576]{1,2,0:T(8,128)(2,1)} %bitcast.61), calls=%async_computation.1 | async-start | bytes 2359296 | tf_op jit(solution)/shard_map/all_to_all | solution.py:487
  198.5 20.3 %copy-start.5 = (bf16[256,576]{0,1:T(8,128)(2,1)}, bf16[256,576]{0,1:T(8,128)(2,1)S(1)}, u32[]{:S(2)}) copy-start(bf16[256,576]{0,1:T(8,128)(2,1)S(1)} %reduce.2) | copy-start | bytes 884740
  238.9 1.3 slice-start
  247.6 19.6 %copy-start.1 = (bf16[2048,64]{0,1:T(8,128)(2,1)S(1)}, bf16[2048,64]{0,1:T(8,128)(2,1)}, u32[]{:S(2)}) copy-start(bf16[2048,64]{0,1:T(8,128)(2,1)} %param.17) | copy-start | bytes 786436
Sparse Core Ops, SparseCore 0:
  25.2 37.1 all-reduce.2
  64.3 68.0 all-gather.3
  155.8 86.7 all-gather.5
